TPU v7x, 8 devices: a whole 2x2x1 slice. The times are simulated.
8 devices in a mesh: side: 2 (over z, y), rep: 4 (over x, core).
Axes of the slice: x: 2, y: 2, z: 1, core: 2. Of those that a mesh axis runs over, the one named last changes fastest.
Arguments:
- w_up: float32 [2, 1, 2048, 8192], P('side', None, 'rep')
- w_down: float32 [2, 1, 8192, 2048], P('side', None, None, 'rep')
- g_up: float32 [2, 1, 2048, 8192], P('side', None, 'rep')
- g_down: float32 [2, 1, 8192, 2048], P('side', None, None, 'rep')
- learn_rate: float32 [1], replicated
- old_up: bfloat16 [2, 4, 1, 2048, 8192], P('side', 'rep')
- old_down: bfloat16 [2, 4, 1, 8192, 2048], P('side', 'rep')
- prompts: bfloat16 [2, 4, 2048, 2048], P('side', 'rep')
Outputs:
- output 1: float32 [2, 1, 2048, 8192], P('side', None, 'rep')
- output 2: float32 [2, 1, 8192, 2048], P('side', None, None, 'rep')
- output 3: bfloat16 [2, 4, 2048, 2048], P('side', 'rep')
All inputs are finite; a program needn't handle non-finite values.
Results may differ from a plain program's by a relative error of at most 0.001.
Values are sent between devices in bfloat16 or wider.
A program may use at most 1 GiB of HBM per device.

v0:
```python
import jax
import jax.numpy as jnp
from jax import lax
from jax.sharding import PartitionSpec as P


def solution(mesh):
    tp_width = mesh.shape["side"] // 2
    send_pairs = [(slot_pos, slot_pos + tp_width) for slot_pos in range(tp_width)]
    up_spec = P("side", None, "rep", None)
    down_spec = P("side", None, None, "rep")
    copy_spec = P("side", "rep", None, None, None)
    token_spec = P("side", "rep", None, None)

    def local_step(w_up, w_down, g_up, g_down, learn_rate, old_up, old_down, prompts):
        step_rate = learn_rate[0]
        new_up = w_up - step_rate * g_up
        new_down = w_down - step_rate * g_down
        delta_up = (new_up - w_up)[0].astype(jnp.bfloat16)
        delta_down = (new_down - w_down)[0].astype(jnp.bfloat16)
        recv_up = lax.ppermute(delta_up, "side", send_pairs)
        recv_down = lax.ppermute(delta_down, "side", send_pairs)
        full_up = lax.all_gather(recv_up, "rep", axis=1, tiled=True)
        full_down = lax.all_gather(recv_down, "rep", axis=2, tiled=True)
        gen_up = (old_up[0, 0].astype(jnp.float32) + full_up.astype(jnp.float32)).astype(jnp.bfloat16)
        gen_down = (old_down[0, 0].astype(jnp.float32) + full_down.astype(jnp.float32)).astype(jnp.bfloat16)
        is_gen = lax.axis_index("side") >= tp_width
        gen_mask = is_gen.astype(jnp.float32)
        hidden = prompts[0, 0]
        for layer_idx in range(w_up.shape[1]):
            pre_act = jnp.dot(hidden, gen_up[layer_idx], preferred_element_type=jnp.float32)
            act_val = jax.nn.gelu(pre_act, approximate=False).astype(jnp.bfloat16)
            part_sum = jnp.dot(act_val, gen_down[layer_idx], preferred_element_type=jnp.float32)
            tp_total = lax.psum(part_sum * gen_mask, "side")
            hidden = (hidden.astype(jnp.float32) + tp_total).astype(jnp.bfloat16)
        y_local = jnp.where(is_gen, hidden, jnp.zeros_like(hidden))
        return new_up, new_down, y_local[None, None]

    return jax.shard_map(
        local_step,
        mesh=mesh,
        in_specs=(up_spec, down_spec, up_spec, down_spec, P(None), copy_spec, copy_spec, token_spec),
        out_specs=(up_spec, down_spec, token_spec),
        check_vma=False,
    )
```

profile of v0, /device:TPU:5, one launch (start us, length us, event | category | flops | bytes accessed | tf_op | source)
XLA Modules:
  0.0 1124.5 jit_solution(13135861528591561318)
XLA Ops:
  7.2 0.0 all-gather.3.cloned.1.call-start
  7.9 17.8 %fusion.33 = (bf16[1,512,8192]{2,1,0:T(8,128)(2,1)S(1)}, f32[1,1,512,8192]{3,2,1,0:T(8,128)}) fusion(f32[1,1,512,8192]{3,2,1,0:T(8,128)} %param.8, f32[1,1,512,8192]{3,2,1,0:T(8,128)} %param.10, f32[]{:T(128)} %bitcast.111), kind=kLoop, calls=%fused_computation.40 | loop fusion | flops 16777216 | bytes 58720260 | tf_op jit(solution)/shard_map/convert_element_type | solution.py:19
  25.6 1.3 collective-permute-start
  26.9 182.0 %collective-permute-done = bf16[1,512,8192]{2,1,0:T(8,128)(2,1)} collective-permute-done((bf16[1,512,8192]{2,1,0:T(8,128)(2,1)S(1)}, bf16[1,512,8192]{2,1,0:T(8,128)(2,1)}, u32[]{:S(2)}, u32[]{:S(2)}) %collective-permute-start) | collective-permute-done | bytes 8388640 | tf_op jit(solution)/shard_map/ppermute | solution.py:21
  209.0 0.0 all-gather.3.cloned.1.call-update
  209.0 0.0 all-gather.5.cloned.1.call-start
  209.0 17.0 %fusion.34 = (bf16[1,8192,512]{2,1,0:T(8,128)(2,1)S(1)}, f32[1,1,8192,512]{3,2,1,0:T(8,128)}) fusion(f32[1,1,8192,512]{3,2,1,0:T(8,128)} %param.9, f32[1,1,8192,512]{3,2,1,0:T(8,128)} %param.11, f32[]{:T(128)} %bitcast.112), kind=kLoop, calls=%fused_computation.41 | loop fusion | flops 16777216 | bytes 58720260 | tf_op jit(solution)/shard_map/convert_element_type | solution.py:20
  226.0 1.3 collective-permute-start.1
  227.3 181.3 %collective-permute-done.1 = bf16[1,8192,512]{2,1,0:T(8,128)(2,1)} collective-permute-done((bf16[1,8192,512]{2,1,0:T(8,128)(2,1)S(1)}, bf16[1,8192,512]{2,1,0:T(8,128)(2,1)}, u32[]{:S(2)}, u32[]{:S(2)}) %collective-permute-start.1) | collective-permute-done | bytes 8388640 | tf_op jit(solution)/shard_map/ppermute | solution.py:22
  408.6 0.0 all-gather.5.cloned.1.call-update
  408.7 0.0 all-reduce.2.cloned.1.call-start
  408.7 1.9 all-gather.3.cloned.1.call-done
  410.6 239.6 %fusion.2 = bf16[2048,8192]{0,1:T(8,128)(2,1)} fusion(bf16[1,2048,8192]{2,1,0:T(8,128)(2,1)} %all-gather.3.cloned.1.call-done, bf16[1,1,1,2048,8192]{4,3,2,1,0:T(8,128)(2,1)} %param.13, bf16[1,1,2048,2048]{3,2,1,0:T(8,128)(2,1)} %param.15), kind=kOutput, calls=%fused_computation.3 | convolution fusion | flops 69877104640 | bytes 109051904 | tf_op jit(solution)/shard_map/dot_general | solution.py:31
  650.2 0.0 all-gather.5.cloned.1.call-done
  650.2 83.3 %fusion.30 = f32[2048,2048]{1,0:T(8,128)} fusion(bf16[2048,8192]{0,1:T(8,128)(2,1)} %fusion.2, bf16[1,8192,2048]{2,1,0:T(8,128)(2,1)} %all-gather.5.cloned.1.call-done, bf16[1,1,1,8192,2048]{4,3,2,1,0:T(8,128)(2,1)} %param.14, f32[]{:T(128)S(6)} %convert_element_type.94), kind=kOutput, calls=%fused_computation.39 | convolution fusion | flops 68790779904 | bytes 117440512 | tf_op jit(solution)/shard_map/dot_general | solution.py:33
  733.5 0.0 all-reduce.2.cloned.1.call-update
  733.6 372.3 %all-reduce.2.cloned.1.call-done = f32[2048,2048]{1,0:T(8,128)} async-done(((f32[2048,2048]{1,0:T(8,128)}), f32[2048,2048]{1,0:T(8,128)}) %all-reduce.2.cloned.1.call-update) | async-done | bytes 16777232 | tf_op jit(solution)/shard_map/psum | solution.py:34
  1105.9 11.9 %fusion.36 = bf16[1,1,2048,2048]{3,2,1,0:T(8,128)(2,1)} fusion(f32[2048,2048]{1,0:T(8,128)} %all-reduce.2.cloned.1.call-done, bf16[1,1,2048,2048]{3,2,1,0:T(8,128)(2,1)} %param.15, pred[]{:T(512)S(6)} %ge.3), kind=kLoop, calls=%fused_computation.43 | loop fusion | flops 16777216 | bytes 33554432 | tf_op jit(solution)/shard_map/broadcast_in_dim | solution.py:37
Async XLA Ops:
  7.2 403.4 %all-gather.3.cloned.1.call-start = ((), (), s32[]{:S(2)}) async-start(), calls=%async_computation | async-start | bytes 41943040 | tf_op jit(solution)/shard_map/all_gather | solution.py:23
  25.6 183.3 %collective-permute-start = (bf16[1,512,8192]{2,1,0:T(8,128)(2,1)S(1)}, bf16[1,512,8192]{2,1,0:T(8,128)(2,1)}, u32[]{:S(2)}, u32[]{:S(2)}) collective-permute-start(bf16[1,512,8192]{2,1,0:T(8,128)(2,1)S(1)} %get-tuple-element.5), channel_id=1, source_target_pairs={{0,4},{1,5},{2,6},{3,7}} | collective-permute-start | bytes 25165832 | tf_op jit(solution)/shard_map/ppermute | solution.py:21
  209.0 441.2 %all-gather.5.cloned.1.call-start = ((), (), s32[]{:S(2)}) async-start(), calls=%async_computation.1 | async-start | bytes 41943040 | tf_op jit(solution)/shard_map/all_gather | solution.py:24
  226.0 182.6 %collective-permute-start.1 = (bf16[1,8192,512]{2,1,0:T(8,128)(2,1)S(1)}, bf16[1,8192,512]{2,1,0:T(8,128)(2,1)}, u32[]{:S(2)}, u32[]{:S(2)}) collective-permute-start(bf16[1,8192,512]{2,1,0:T(8,128)(2,1)S(1)} %get-tuple-element.3), channel_id=1, source_target_pairs={{0,4},{1,5},{2,6},{3,7}} | collective-permute-start | bytes 25165832 | tf_op jit(solution)/shard_map/ppermute | solution.py:22
  408.7 697.3 %all-reduce.2.cloned.1.call-start = ((), (), s32[]{:S(2)}) async-start(), calls=%async_computation.2 | async-start | bytes 33554432 | tf_op jit(solution)/shard_map/psum | solution.py:34
Sparse Core Ops, SparseCore 0:
  209.1 201.4 all-gather.2
  412.1 199.3 all-gather.4
  733.7 372.1 all-reduce.1
where the time goes:
time: 1130 us; the launch traced here: 1120 us
  waiting for transfers between devices  738 us (65%)
  matrix products  323 us (29%)
  other arithmetic  46.7 us (4%)
  between operations  14.6 us (1%)
    psum x1, waiting for transfers between devices, local_step(): tp_total = lax.psum(part_sum * gen_mask, 'side')  372 us
    dot_general x1, matrix products, local_step(): jnp.dot(hidden, gen_up[layer_idx], preferred_element_type=jnp.float32)  240 us
    ppermute x1, waiting for transfers between devices, local_step(): recv_up = lax.ppermute(delta_up, 'side', send_pairs)  182 us
    ppermute x1, waiting for transfers between devices, local_step(): recv_down = lax.ppermute(delta_down, 'side', send_pairs)  181 us
    dot_general x1, matrix products, local_step(): jnp.dot(act_val, gen_down[layer_idx], preferred_element_type=jnp.float32)  83.3 us
  transfers between devices with their start and end apart: 5, of which 4 were waited for; matrix products, arithmetic and copies ran while one was open for 23% of the time, Pallas kernels for 0%

commit v1 on v0

v1 whole, which is shorter than its diff:
```python
import functools

import jax
import jax.numpy as jnp
from jax import lax
from jax.experimental import pallas as pl
from jax.experimental.pallas import tpu as pltpu
from jax.sharding import PartitionSpec as P

MESH = pl.DeviceIdType.MESH
COLS = 256
SENDS = 4
TILE = 512


def gelu(x):
    return 0.5 * x * (1.0 + lax.erf(x * 0.7071067811865476))


def sync_kernel(lr, w_up, w_dn, g_up, g_dn, s_up, s_dn, x_hbm, y_hbm, land_up, land_dn,
                wb_up, wb_dn, gb_up, gb_dn, d_up, d_dn,
                x_v, acc, sb_up, sb_dn, lb_up, lb_dn, wg_up, wg_dn, u_v,
                t_sem, send_sem, s_sem, l_sem, x_sem, y_recv, x_recv, o_recv, n_recv, x_send, o_send, n_send):
    side, rep = lax.axis_index("side"), lax.axis_index("rep")
    other = 1 - side
    sib = rep + 1 - 2 * (rep % 2)
    cross = (rep + 2) % 4
    chunks = land_up.shape[0]
    depth = w_up.shape[0]
    lands, smalls = (land_up, land_dn), (d_up, d_dn)

    barrier = pltpu.get_barrier_semaphore()
    for dev in ((other, rep), (side, sib), (side, cross)):
        pl.semaphore_signal(barrier, inc=1, device_id=dev, device_id_type=MESH)
    pl.semaphore_wait(barrier, 3)

    def span(m):
        return pl.ds(pl.multiple_of(m * COLS, COLS), COLS)

    @pl.when(side == 0)
    def trainer():
        def loads(m):
            k = m % 2
            return [
                pltpu.make_async_copy(w_up.at[:, span(m)], wb_up.at[k], t_sem.at[0, k]),
                pltpu.make_async_copy(g_up.at[:, span(m)], gb_up.at[k], t_sem.at[1, k]),
                pltpu.make_async_copy(w_dn.at[span(m), :], wb_dn.at[k], t_sem.at[2, k]),
                pltpu.make_async_copy(g_dn.at[span(m), :], gb_dn.at[k], t_sem.at[3, k]),
            ]

        def send(h, m):
            return pltpu.make_async_remote_copy(
                src_ref=smalls[h].at[m % SENDS], dst_ref=lands[h].at[m, rep],
                send_sem=send_sem.at[h, m % SENDS], recv_sem=y_recv.at[h, m],
                device_id=(other, rep), device_id_type=MESH)

        for m in range(2):
            for c in loads(m):
                c.start()
        rate = lr[0]

        def step(m, _):
            k = m % 2
            for c in loads(m):
                c.wait()

            @pl.when(m >= SENDS)
            def _():
                for h in range(2):
                    send(h, m - SENDS).wait_send()

            for w, g, d in ((wb_up, gb_up, d_up), (wb_dn, gb_dn, d_dn)):
                old = w[k]
                d[m % SENDS] = ((old - rate * g[k]) - old).astype(jnp.bfloat16)

            @pl.when(m + 2 < chunks)
            def _():
                for c in loads(m + 2):
                    c.start()

            @pl.when(m >= 1)
            def _():
                for h in range(2):
                    send(h, m - 1).start()
            return 0

        lax.fori_loop(0, chunks, step, 0)
        for h in range(2):
            send(h, chunks - 1).start()
        for m in range(chunks - SENDS, chunks):
            for h in range(2):
                send(h, m).wait_send()

    @pl.when(side == 1)
    def generator():
        def hop(h, m, row, dev, send, recv):
            return pltpu.make_async_remote_copy(
                src_ref=lands[h].at[m, row], dst_ref=lands[h].at[m, row],
                send_sem=send.at[h, m], recv_sem=recv.at[h, m],
                device_id=(side, dev), device_id_type=MESH)

        def from_trainer(h, m):
            return hop(h, m, rep, sib, x_send, y_recv)

        def across(h, m, row):
            return hop(h, m, row, cross, x_send, x_recv)

        def own(h, m, row):
            return hop(h, m, row, sib, o_send, o_recv)

        def next_own(h, m, row):
            return hop(h, m, row, sib, n_send, n_recv)

        sib_cross = (sib + 2) % 4
        stales = ((s_up, sb_up), (s_dn, sb_dn))

        def stale(h, m):
            src = s_up.at[:, span(m)] if h == 0 else s_dn.at[span(m), :]
            return pltpu.make_async_copy(src, stales[h][1].at[m % 2], s_sem.at[h, m % 2])

        def landed(h, m):
            return pltpu.make_async_copy(lands[h].at[m], (lb_up, lb_dn)[h].at[m % 2], l_sem.at[h, m % 2])

        x_in = pltpu.make_async_copy(x_hbm, x_v, x_sem.at[0])
        x_in.start()
        for m in range(2):
            for h in range(2):
                stale(h, m).start()
        acc[...] = jnp.zeros_like(acc)
        x_in.wait()

        def route(h, m):
            @pl.when(m < chunks)
            def _():
                from_trainer(h, m).wait_recv()
                across(h, m, rep).start()
                own(h, m, rep).start()

            @pl.when((m >= 1) & (m < chunks + 1))
            def _():
                across(h, m - 1, cross).wait_recv()
                next_own(h, m - 1, cross).start()

            @pl.when((m >= 2) & (m < chunks + 2))
            def _():
                own(h, m - 2, sib).wait_recv()
                next_own(h, m - 2, sib_cross).wait_recv()
                landed(h, m - 2).start()

        def up(m):
            k = m % 2
            landed(0, m).wait()
            stale(0, m).wait()
            for r in range(4):
                rows = pl.ds(r * depth, depth)
                wg_up[rows, :] = (sb_up[k, rows, :].astype(jnp.float32) + lb_up[k, r].astype(jnp.float32)).astype(jnp.bfloat16)

            @pl.when(m + 2 < chunks)
            def _():
                stale(0, m + 2).start()

            def tile(i, _):
                rows = pl.ds(pl.multiple_of(i * TILE, TILE), TILE)
                pre = jnp.dot(x_v[rows, :], wg_up[...], preferred_element_type=jnp.float32)
                u_v[rows, :] = gelu(pre).astype(jnp.bfloat16)
                return 0
            lax.fori_loop(0, x_v.shape[0] // TILE, tile, 0)

        def down(m):
            k = m % 2
            landed(1, m).wait()
            stale(1, m).wait()
            for r in range(4):
                cols = pl.ds(r * depth, depth)
                wg_dn[:, cols] = (sb_dn[k, :, cols].astype(jnp.float32) + lb_dn[k, r].astype(jnp.float32)).astype(jnp.bfloat16)

            @pl.when(m + 2 < chunks)
            def _():
                stale(1, m + 2).start()

            def tile(i, _):
                rows = pl.ds(pl.multiple_of(i * TILE, TILE), TILE)
                acc[rows, :] += jnp.dot(u_v[rows, :], wg_dn[...], preferred_element_type=jnp.float32)
                return 0
            lax.fori_loop(0, x_v.shape[0] // TILE, tile, 0)

        def step(m, _):
            route(0, m)

            @pl.when(m >= 3)
            def _():
                down(m - 3)
            route(1, m)

            @pl.when((m >= 2) & (m < chunks + 2))
            def _():
                up(m - 2)
            return 0

        lax.fori_loop(0, chunks + 3, step, 0)

        def finish(i, _):
            rows = pl.ds(pl.multiple_of(i * TILE, TILE), TILE)
            x_v[rows, :] = (x_v[rows, :].astype(jnp.float32) + acc[rows, :]).astype(jnp.bfloat16)
            return 0
        lax.fori_loop(0, x_v.shape[0] // TILE, finish, 0)
        out = pltpu.make_async_copy(x_v, y_hbm, x_sem.at[0])
        out.start()

        def drain(m, _):
            for h in range(2):
                across(h, m, rep).wait_send()
                own(h, m, rep).wait_send()
                next_own(h, m, cross).wait_send()
            return 0
        lax.fori_loop(0, chunks, drain, 0)
        out.wait()


def synced_output(lr, w_up, w_dn, g_up, g_dn, s_up, s_dn, x):
    depth, hid = w_up.shape
    tokens, width = x.shape
    chunks = hid // COLS
    any_spec = pl.BlockSpec(memory_space=pltpu.HBM)
    dma = pltpu.SemaphoreType.DMA
    y, _, _ = pl.pallas_call(
        sync_kernel,
        name="sync_kernel",
        out_shape=(
            jax.ShapeDtypeStruct((tokens, width), jnp.bfloat16),
            jax.ShapeDtypeStruct((chunks, 4, depth, COLS), jnp.bfloat16),
            jax.ShapeDtypeStruct((chunks, 4, COLS, depth), jnp.bfloat16),
        ),
        in_specs=[pl.BlockSpec(memory_space=pltpu.SMEM)] + [any_spec] * 7,
        out_specs=(any_spec,) * 3,
        scratch_shapes=[
            pltpu.VMEM((2, depth, COLS), jnp.float32),
            pltpu.VMEM((2, COLS, depth), jnp.float32),
            pltpu.VMEM((2, depth, COLS), jnp.float32),
            pltpu.VMEM((2, COLS, depth), jnp.float32),
            pltpu.VMEM((SENDS, depth, COLS), jnp.bfloat16),
            pltpu.VMEM((SENDS, COLS, depth), jnp.bfloat16),
            pltpu.VMEM((tokens, width), jnp.bfloat16),
            pltpu.VMEM((tokens, width), jnp.float32),
            pltpu.VMEM((2, width, COLS), jnp.bfloat16),
            pltpu.VMEM((2, COLS, width), jnp.bfloat16),
            pltpu.VMEM((2, 4, depth, COLS), jnp.bfloat16),
            pltpu.VMEM((2, 4, COLS, depth), jnp.bfloat16),
            pltpu.VMEM((width, COLS), jnp.bfloat16),
            pltpu.VMEM((COLS, width), jnp.bfloat16),
            pltpu.VMEM((tokens, COLS), jnp.bfloat16),
            dma((4, 2)), dma((2, SENDS)), dma((2, 2)), dma((2, 2)), dma((1,)),
        ] + [dma((2, chunks))] * 7,
        compiler_params=pltpu.CompilerParams(
            collective_id=0, has_side_effects=True, vmem_limit_bytes=62 * 1024 * 1024),
        cost_estimate=pl.CostEstimate(flops=4 * tokens * width * hid, bytes_accessed=8 * width * hid, transcendentals=0),
    )(lr, w_up, w_dn, g_up, g_dn, s_up, s_dn, x)
    return y


def solution(mesh):
    tp_width = mesh.shape["side"] // 2
    up_spec = P("side", None, "rep", None)
    down_spec = P("side", None, None, "rep")
    copy_spec = P("side", "rep", None, None, None)
    token_spec = P("side", "rep", None, None)

    def local_step(w_up, w_down, g_up, g_down, learn_rate, old_up, old_down, prompts):
        y = synced_output(learn_rate, w_up[0, 0], w_down[0, 0], g_up[0, 0], g_down[0, 0],
                          old_up[0, 0, 0], old_down[0, 0, 0], prompts[0, 0])
        is_gen = lax.axis_index("side") >= tp_width
        step_rate = learn_rate[0]
        new_up = w_up - step_rate * g_up
        new_down = w_down - step_rate * g_down
        y_local = jnp.where(is_gen, y, jnp.zeros_like(y))
        return new_up, new_down, y_local[None, None]

    return jax.shard_map(
        local_step,
        mesh=mesh,
        in_specs=(up_spec, down_spec, up_spec, down_spec, P(None), copy_spec, copy_spec, token_spec),
        out_specs=(up_spec, down_spec, token_spec),
        check_vma=False,
    )
```

time: 1130 us -> 434 us (0.38)
  waiting for transfers between devices: 738 us -> 0 us
  Pallas kernels: 0 us -> 392 us
  matrix products: 323 us -> 0 us
  between operations: 14.6 us -> 1.3 us
    pallas_call x0 -> x1, Pallas kernels: none -> 392 us  [synced_output(): pl.pallas_call(sync_kernel, name='sync_kernel', out_shape=(jax.ShapeDtype...]
    psum x1 -> x0, waiting for transfers between devices: 372 us -> none  [local_step(): tp_total = lax.psum(part_sum * gen_mask, 'side')]
    ppermute x2 -> x0, waiting for transfers between devices: 363 us -> none  [the longest x1 182 us: local_step(): recv_up = lax.ppermute(delta_up, 'side', send_pairs)]
    dot_general x2 -> x0, matrix products: 323 us -> none  [the longest x1 240 us: local_step(): jnp.dot(hidden, gen_up[layer_idx], preferred_element_type=jnp.float32)]
    convert_element_type x2 -> x0, other arithmetic: 34.8 us -> none  [the longest x1 17.8 us: local_step(): delta_up = (new_up - w_up)[0].astype(jnp.bfloat16)]
    sub x0 -> x2, other arithmetic: none -> 29.9 us  [the longest x1 18 us: local_step(): new_down = w_down - step_rate * g_down]
  transfers between devices with their start and end apart: 5 -> 0, of which waited for: 4 -> 0; matrix products, arithmetic and copies ran while one was open for 23% -> 0% of each run, Pallas kernels for 0% -> 0%
where the time goes in v1:
time: 434 us; the launch traced here: 433 us
  Pallas kernels  392 us (90%)
  other arithmetic  37.4 us (9%)
    pallas_call x1, Pallas kernels, synced_output(): pl.pallas_call(sync_kernel, name='sync_kernel', out_shape=(jax.ShapeDtype...  392 us
    sub x1, other arithmetic, local_step(): new_down = w_down - step_rate * g_down  18 us
    sub x1, other arithmetic, local_step(): new_up = w_up - step_rate * g_up  11.9 us

profile of v1, /device:TPU:5, one launch (start us, length us, event | category | flops | bytes accessed | tf_op | source)
XLA Modules:
  0.0 432.6 jit_solution(1448648756626314508)
XLA Ops:
  1.3 391.6 %sync_kernel.1 = (bf16[2048,2048]{1,0:T(8,128)(2,1)}, bf16[32,4,512,256]{3,2,1,0:T(8,128)(2,1)}, bf16[32,4,256,512]{3,2,1,0:T(8,128)(2,1)}) custom-call(f32[1]{0:T(128)} %copy.11.lr, f32[512,8192]{1,0:T(8,128)} %bitcast.14, f32[8192,512]{1,0:T(8,128)} %bitcast.12, f32[512,8192]{1,0:T(8,128)} %bitcast.17, f32[8192,512]{1,0:T(8,128)} %bitcast.13, ...), custom_call_target="tpu_custom_call" | custom-call | flops 137438953472 | bytes 134217728 | tf_op jit(solution)/shard_map/sync_kernel/pallas_call | solution.py:226
  392.9 0.0 slice-start
  392.9 7.5 %select_bitcast_fusion = bf16[1,1,2048,2048]{3,2,1,0:T(8,128)(2,1)} fusion(bf16[2048,2048]{1,0:T(8,128)(2,1)} %get-tuple-element.4, pred[]{:T(512)S(6)} %ge.3), kind=kLoop, calls=%fused_computation.2 | loop fusion | flops 4194304 | bytes 16777216 | tf_op jit(solution)/shard_map/broadcast_in_dim | solution.py:276
  400.4 0.0 slice-start.1
  400.4 0.0 slice-start.2
  400.4 0.0 slice-start.3
  400.4 18.0 %multiply_subtract_fusion = f32[1,1,8192,512]{3,2,1,0:T(8,128)} fusion(f32[1,1,8192,512]{3,2,1,0:T(8,128)} %param.9, f32[1,1,8192,512]{3,2,1,0:T(8,128)} %param.11, f32[]{:T(128)} %bitcast.11), kind=kLoop, calls=%fused_computation | loop fusion | flops 8388608 | bytes 50331652 | tf_op jit(solution)/shard_map/sub | solution.py:274
  418.4 0.0 slice-done
  418.4 0.0 slice-done.1
  418.4 1.1 slice-done.2
  419.5 1.2 slice-done.3
  420.7 11.9 %multiply_subtract_fusion.1 = f32[1,1,512,8192]{3,2,1,0:T(8,128)} fusion(f32[1,1,512,8192]{3,2,1,0:T(8,128)S(1)} %bitcast.16, f32[1,1,512,8192]{3,2,1,0:T(8,128)} %param.10, f32[]{:T(128)} %bitcast.10), kind=kLoop, calls=%fused_computation.1 | loop fusion | flops 8388608 | bytes 50331652 | tf_op jit(solution)/shard_map/sub | solution.py:273
  (1 shorter events, 0.0 us)
Async XLA Ops:
  392.9 25.5 %slice-start = ((s8[16777216]{0:T(1024)(128)(4,1)}), s8[4194304]{0:T(1024)(128)(4,1)S(1)}, s32[]{:S(2)}) async-start(s8[16777216]{0:T(1024)(128)(4,1)} %bitcast.15), calls=%async_computation | async-start | bytes 8388608
  400.4 18.0 %slice-start.1 = ((s8[16777216]{0:T(1024)(128)(4,1)}), s8[4194304]{0:T(1024)(128)(4,1)S(1)}, s32[]{:S(2)}) async-start(s8[16777216]{0:T(1024)(128)(4,1)} %bitcast.15), calls=%async_computation.1 | async-start | bytes 8388608
  400.4 19.1 %slice-start.2 = ((s8[16777216]{0:T(1024)(128)(4,1)}), s8[4194304]{0:T(1024)(128)(4,1)S(1)}, s32[]{:S(2)}) async-start(s8[16777216]{0:T(1024)(128)(4,1)} %bitcast.15), calls=%async_computation.2 | async-start | bytes 8388608
  400.4 20.3 %slice-start.3 = ((s8[16777216]{0:T(1024)(128)(4,1)}), s8[4194304]{0:T(1024)(128)(4,1)S(1)}, s32[]{:S(2)}) async-start(s8[16777216]{0:T(1024)(128)(4,1)} %bitcast.15), calls=%async_computation.3 | async-start | bytes 8388608

commit v2 on v1

v2 whole, which is shorter than its diff:
```python
import functools

import jax
import jax.numpy as jnp
from jax import lax
from jax.experimental import pallas as pl
from jax.experimental.pallas import tpu as pltpu
from jax.sharding import PartitionSpec as P

MESH = pl.DeviceIdType.MESH
COLS = 256
SENDS = 4
TILE = 512


def gelu(x):
    return 0.5 * x * (1.0 + lax.erf(x * 0.7071067811865476))


def sync_kernel(lr, w_up, w_dn, g_up, g_dn, s_up, s_dn, x_hbm, y_hbm, land_up, land_dn, nw_up, nw_dn,
                wb_up, wb_dn, gb_up, gb_dn, d_up, d_dn, nb_up, nb_dn,
                x_v, acc, sb_up, sb_dn, lb_up, lb_dn, wg_up, wg_dn, u_v,
                t_sem, w_sem, send_sem, s_sem, l_sem, x_sem, out_sem,
                y_recv, x_recv, o_recv, n_recv, x_send, o_send, n_send):
    side, rep = lax.axis_index("side"), lax.axis_index("rep")
    other = 1 - side
    sib = rep + 1 - 2 * (rep % 2)
    cross = (rep + 2) % 4
    chunks = land_up.shape[0]
    depth = w_up.shape[0]
    lands, smalls = (land_up, land_dn), (d_up, d_dn)

    barrier = pltpu.get_barrier_semaphore()
    for dev in ((other, rep), (side, sib), (side, cross)):
        pl.semaphore_signal(barrier, inc=1, device_id=dev, device_id_type=MESH)

    def span(m):
        return pl.ds(pl.multiple_of(m * COLS, COLS), COLS)

    @pl.when(side == 0)
    def trainer():
        mats = ((w_up, g_up, wb_up, gb_up, nb_up, nw_up), (w_dn, g_dn, wb_dn, gb_dn, nb_dn, nw_dn))

        def part(h, ref, m):
            return ref.at[:, span(m)] if h == 0 else ref.at[span(m), :]

        def loads(h, m):
            w, g, wb, gb, _, _ = mats[h]
            k = m % 2
            return [
                pltpu.make_async_copy(part(h, w, m), wb.at[k], t_sem.at[2 * h, k]),
                pltpu.make_async_copy(part(h, g, m), gb.at[k], t_sem.at[2 * h + 1, k]),
            ]

        def store(h, m):
            return pltpu.make_async_copy(mats[h][4].at[m % 2], part(h, mats[h][5], m), w_sem.at[h, m % 2])

        def send(h, m):
            return pltpu.make_async_remote_copy(
                src_ref=smalls[h].at[m % SENDS], dst_ref=lands[h].at[m, rep],
                send_sem=send_sem.at[h, m % SENDS], recv_sem=y_recv.at[h, m],
                device_id=(other, rep), device_id_type=MESH)

        for m in range(2):
            for h in range(2):
                for c in loads(h, m):
                    c.start()
        rate = lr[0]

        def make(h, m):
            _, _, wb, gb, nb, _ = mats[h]
            k = m % 2
            for c in loads(h, m):
                c.wait()

            @pl.when(m >= SENDS)
            def _():
                send(h, m - SENDS).wait_send()

            @pl.when(m >= 2)
            def _():
                store(h, m - 2).wait()
            old = wb[k]
            new = old - rate * gb[k]
            nb[k] = new
            smalls[h][m % SENDS] = (new - old).astype(jnp.bfloat16)

            @pl.when(m + 2 < chunks)
            def _():
                for c in loads(h, m + 2):
                    c.start()

        make(0, 0)
        pl.semaphore_wait(barrier, 3)

        def step(m, _):
            @pl.when(m + 1 < chunks)
            def _():
                make(0, m + 1)

            @pl.when(m == 0)
            def _():
                send(0, 0).start()
                store(0, 0).start()

            @pl.when(m >= 1)
            def _():
                send(1, m - 1).start()
                store(1, m - 1).start()
            make(1, m)

            @pl.when(m + 1 < chunks)
            def _():
                send(0, m + 1).start()
                store(0, m + 1).start()
            return 0

        lax.fori_loop(0, chunks, step, 0)
        send(1, chunks - 1).start()
        store(1, chunks - 1).start()
        for h in range(2):
            for m in range(chunks - 2, chunks):
                store(h, m).wait()
        for m in range(chunks - SENDS, chunks):
            for h in range(2):
                send(h, m).wait_send()

    @pl.when(side == 1)
    def generator():
        def hop(h, m, row, dev, send, recv):
            return pltpu.make_async_remote_copy(
                src_ref=lands[h].at[m, row], dst_ref=lands[h].at[m, row],
                send_sem=send.at[h, m], recv_sem=recv.at[h, m],
                device_id=(side, dev), device_id_type=MESH)

        def from_trainer(h, m):
            return hop(h, m, rep, sib, x_send, y_recv)

        def across(h, m, row):
            return hop(h, m, row, cross, x_send, x_recv)

        def own(h, m, row):
            return hop(h, m, row, sib, o_send, o_recv)

        def next_own(h, m, row):
            return hop(h, m, row, sib, n_send, n_recv)

        sib_cross = (sib + 2) % 4
        stales = (sb_up, sb_dn)

        def stale(h, m):
            src = s_up.at[:, span(m)] if h == 0 else s_dn.at[span(m), :]
            return pltpu.make_async_copy(src, stales[h].at[m % 2], s_sem.at[h, m % 2])

        def landed(h, m):
            return pltpu.make_async_copy(lands[h].at[m], (lb_up, lb_dn)[h], l_sem.at[h])

        x_in = pltpu.make_async_copy(x_hbm, x_v, x_sem.at[0])
        x_in.start()
        for m in range(2):
            for h in range(2):
                stale(h, m).start()
        acc[...] = jnp.zeros_like(acc)
        x_in.wait()
        pl.semaphore_wait(barrier, 3)

        def pass_on(h, m):
            from_trainer(h, m).wait_recv()
            across(h, m, rep).start()
            own(h, m, rep).start()

        def turn(h, m):
            across(h, m, cross).wait_recv()
            next_own(h, m, cross).start()

        def fetch(h, m):
            own(h, m, sib).wait_recv()
            next_own(h, m, sib_cross).wait_recv()
            landed(h, m).start()

        tiles = x_v.shape[0] // TILE

        def up(m):
            k = m % 2
            stale(0, m).wait()
            landed(0, m).wait()
            for r in range(4):
                rows = pl.ds(r * depth, depth)
                wg_up[rows, :] = (sb_up[k, rows, :].astype(jnp.float32) + lb_up[r].astype(jnp.float32)).astype(jnp.bfloat16)

            @pl.when(m + 2 < chunks)
            def _():
                stale(0, m + 2).start()

            def tile(i, _):
                rows = pl.ds(pl.multiple_of(i * TILE, TILE), TILE)
                pre = jnp.dot(x_v[rows, :], wg_up[...], preferred_element_type=jnp.float32)
                u_v[k, rows, :] = gelu(pre).astype(jnp.bfloat16)
                return 0
            lax.fori_loop(0, tiles, tile, 0)

        def down_weights(m):
            k = m % 2
            stale(1, m).wait()
            landed(1, m).wait()
            for r in range(4):
                cols = pl.ds(r * depth, depth)
                wg_dn[:, cols] = (sb_dn[k, :, cols].astype(jnp.float32) + lb_dn[r].astype(jnp.float32)).astype(jnp.bfloat16)

        def down(m):
            down_weights(m)

            @pl.when(m + 2 < chunks)
            def _():
                stale(1, m + 2).start()

            def tile(i, _):
                rows = pl.ds(pl.multiple_of(i * TILE, TILE), TILE)
                acc[rows, :] += jnp.dot(u_v[m % 2, rows, :], wg_dn[...], preferred_element_type=jnp.float32)
                return 0
            lax.fori_loop(0, tiles, tile, 0)

        pass_on(0, 0)

        def step(m, _):
            pass_on(0, m)
            turn(0, m - 1)

            @pl.when(m >= 3)
            def _():
                down(m - 3)
            fetch(0, m - 1)
            pass_on(1, m - 1)

            @pl.when(m >= 2)
            def _():
                turn(1, m - 2)
            up(m - 1)

            @pl.when(m >= 2)
            def _():
                fetch(1, m - 2)
            return 0

        lax.fori_loop(1, chunks, step, 0)
        last = chunks - 1
        turn(0, last)
        down(last - 2)
        fetch(0, last)
        pass_on(1, last)
        up(last)
        turn(1, last - 1)
        fetch(1, last - 1)
        down(last - 1)
        turn(1, last)
        fetch(1, last)
        down_weights(last)

        def y_out(i):
            rows = pl.ds(pl.multiple_of(i * TILE, TILE), TILE)
            return pltpu.make_async_copy(x_v.at[rows, :], y_hbm.at[rows, :], out_sem.at[i])

        def tile(i, _):
            rows = pl.ds(pl.multiple_of(i * TILE, TILE), TILE)
            p = acc[rows, :] + jnp.dot(u_v[last % 2, rows, :], wg_dn[...], preferred_element_type=jnp.float32)
            x_v[rows, :] = (x_v[rows, :].astype(jnp.float32) + p).astype(jnp.bfloat16)

            @pl.when(i >= 1)
            def _():
                y_out(i - 1).start()
            return 0
        lax.fori_loop(0, tiles, tile, 0)

        def drain(m, _):
            for h in range(2):
                across(h, m, rep).wait_send()
                own(h, m, rep).wait_send()
                next_own(h, m, cross).wait_send()
            return 0
        lax.fori_loop(0, chunks, drain, 0)
        y_out(tiles - 1).start()
        for i in range(tiles):
            y_out(i).wait()


def finish_kernel(y_hbm, nw_up, nw_dn, new_up, new_dn, y_out, b_up, b_dn, b_y, in_sem, out_sem):
    side = lax.axis_index("side")
    n, rows, cols = b_up.shape
    ny = b_y.shape[0]
    row_y = b_y.shape[1]

    def piece(ref, h, i):
        return ref.at[:, pl.ds(i * cols, cols)] if h == 0 else ref.at[pl.ds(i * cols, cols), :]

    def y_piece(ref, i):
        return ref.at[pl.ds(i * row_y, row_y), :]

    mats = ((nw_up, b_up, new_up), (nw_dn, b_dn, new_dn))

    @pl.when(side == 0)
    def trainer():
        def read(h, i):
            return pltpu.make_async_copy(piece(mats[h][0], h, i), mats[h][1].at[i], in_sem.at[h, i])

        def write(h, i):
            return pltpu.make_async_copy(mats[h][1].at[i], piece(mats[h][2], h, i), out_sem.at[h, i])

        def write_y(i):
            return pltpu.make_async_copy(b_y.at[0], y_piece(y_out, i), out_sem.at[2, i])

        for i in range(n):
            for h in range(2):
                read(h, i).start()
        b_y[0] = jnp.zeros_like(b_y[0])
        for i in range(n):
            for h in range(2):
                read(h, i).wait()
                write(h, i).start()
        for i in range(ny):
            write_y(i).start()
        for i in range(n):
            for h in range(2):
                write(h, i).wait()
        for i in range(ny):
            write_y(i).wait()

    @pl.when(side == 1)
    def generator():
        def write(h, i):
            return pltpu.make_async_copy(mats[h][1].at[0], piece(mats[h][2], h, i), out_sem.at[h, i])

        def read_y(i):
            return pltpu.make_async_copy(y_piece(y_hbm, i), b_y.at[i], in_sem.at[2, i])

        def write_y(i):
            return pltpu.make_async_copy(b_y.at[i], y_piece(y_out, i), out_sem.at[2, i])

        for i in range(ny):
            read_y(i).start()
        b_up[0] = jnp.zeros_like(b_up[0])
        b_dn[0] = jnp.zeros_like(b_dn[0])
        for i in range(ny):
            read_y(i).wait()
            write_y(i).start()
        for i in range(n):
            for h in range(2):
                write(h, i).start()
        for i in range(n):
            for h in range(2):
                write(h, i).wait()
        for i in range(ny):
            write_y(i).wait()


def step_outputs(lr, w_up, w_dn, g_up, g_dn, s_up, s_dn, x):
    depth, hid = w_up.shape
    tokens, width = x.shape
    chunks = hid // COLS
    any_spec = pl.BlockSpec(memory_space=pltpu.HBM)
    dma = pltpu.SemaphoreType.DMA
    vmem = pltpu.VMEM
    f32, bf16 = jnp.float32, jnp.bfloat16
    y, _, _, nw_up, nw_dn = pl.pallas_call(
        sync_kernel,
        name="sync_kernel",
        out_shape=(
            jax.ShapeDtypeStruct((tokens, width), bf16),
            jax.ShapeDtypeStruct((chunks, 4, depth, COLS), bf16),
            jax.ShapeDtypeStruct((chunks, 4, COLS, depth), bf16),
            jax.ShapeDtypeStruct(w_up.shape, f32),
            jax.ShapeDtypeStruct(w_dn.shape, f32),
        ),
        in_specs=[pl.BlockSpec(memory_space=pltpu.SMEM)] + [any_spec] * 7,
        out_specs=(any_spec,) * 5,
        scratch_shapes=[
            vmem((2, depth, COLS), f32), vmem((2, COLS, depth), f32),
            vmem((2, depth, COLS), f32), vmem((2, COLS, depth), f32),
            vmem((SENDS, depth, COLS), bf16), vmem((SENDS, COLS, depth), bf16),
            vmem((2, depth, COLS), f32), vmem((2, COLS, depth), f32),
            vmem((tokens, width), bf16), vmem((tokens, width), f32),
            vmem((2, width, COLS), bf16), vmem((2, COLS, width), bf16),
            vmem((4, depth, COLS), bf16), vmem((4, COLS, depth), bf16),
            vmem((width, COLS), bf16), vmem((COLS, width), bf16),
            vmem((2, tokens, COLS), bf16),
            dma((4, 2)), dma((2, 2)), dma((2, SENDS)), dma((2, 2)), dma((2,)), dma((1,)), dma((tokens // TILE,)),
        ] + [dma((2, chunks))] * 7,
        compiler_params=pltpu.CompilerParams(
            collective_id=0, has_side_effects=True, vmem_limit_bytes=60 * 1024 * 1024),
        cost_estimate=pl.CostEstimate(flops=4 * tokens * width * hid, bytes_accessed=8 * width * hid, transcendentals=0),
    )(lr, w_up, w_dn, g_up, g_dn, s_up, s_dn, x)
    piece = 1024
    return pl.pallas_call(
        finish_kernel,
        name="finish_kernel",
        out_shape=(
            jax.ShapeDtypeStruct(w_up.shape, f32),
            jax.ShapeDtypeStruct(w_dn.shape, f32),
            jax.ShapeDtypeStruct((tokens, width), bf16),
        ),
        in_specs=[any_spec] * 3,
        out_specs=(any_spec,) * 3,
        scratch_shapes=[
            vmem((hid // piece, depth, piece), f32), vmem((hid // piece, piece, depth), f32),
            vmem((4, tokens // 4, width), bf16),
            dma((3, hid // piece)), dma((3, hid // piece)),
        ],
        compiler_params=pltpu.CompilerParams(vmem_limit_bytes=60 * 1024 * 1024),
        cost_estimate=pl.CostEstimate(flops=0, bytes_accessed=20 * depth * hid, transcendentals=0),
    )(y, nw_up, nw_dn)


def solution(mesh):
    up_spec = P("side", None, "rep", None)
    down_spec = P("side", None, None, "rep")
    copy_spec = P("side", "rep", None, None, None)
    token_spec = P("side", "rep", None, None)

    def local_step(w_up, w_down, g_up, g_down, learn_rate, old_up, old_down, prompts):
        new_up, new_down, y = step_outputs(
            learn_rate, w_up[0, 0], w_down[0, 0], g_up[0, 0], g_down[0, 0],
            old_up[0, 0, 0], old_down[0, 0, 0], prompts[0, 0])
        return new_up[None, None], new_down[None, None], y[None, None]

    return jax.shard_map(
        local_step,
        mesh=mesh,
        in_specs=(up_spec, down_spec, up_spec, down_spec, P(None), copy_spec, copy_spec, token_spec),
        out_specs=(up_spec, down_spec, token_spec),
        check_vma=False,
    )
```

time: 434 us -> 406 us (0.935)
  other arithmetic: 37.4 us -> 0 us
  Pallas kernels: 392 us -> 404 us
    sub x2 -> x0, other arithmetic: 29.9 us -> none  [the longest x1 18 us: local_step(): new_down = w_down - step_rate * g_down]
    pallas_call x1 -> x2, Pallas kernels: 392 us -> 404 us  [the longest x1 386 us: step_outputs(): pl.pallas_call(sync_kernel, name='sync_kernel', out_shape=(jax.ShapeDtype...]
    broadcast_in_dim x1 -> x0, other arithmetic: 7.48 us -> none  [local_step(): return (new_up, new_down, y_local[None, None])]
where the time goes in v2:
time: 406 us; the launch traced here: 405 us
  Pallas kernels  404 us (100%)
    pallas_call x1, Pallas kernels, step_outputs(): pl.pallas_call(sync_kernel, name='sync_kernel', out_shape=(jax.ShapeDtype...  386 us
    pallas_call x1, Pallas kernels, step_outputs(): pl.pallas_call(finish_kernel, name='finish_kernel', out_shape=(jax.ShapeD...  17.5 us

profile of v2, /device:TPU:5, one launch (start us, length us, event | category | flops | bytes accessed | tf_op | source)
XLA Modules:
  0.0 404.9 jit_solution(18379507650592504049)
XLA Ops:
  1.3 386.1 %sync_kernel.1 = (bf16[2048,2048]{1,0:T(8,128)(2,1)}, bf16[32,4,512,256]{3,2,1,0:T(8,128)(2,1)}, bf16[32,4,256,512]{3,2,1,0:T(8,128)(2,1)}, f32[512,8192]{1,0:T(8,128)}, f32[8192,512]{1,0:T(8,128)}) custom-call(f32[1]{0:T(128)S(6)} %copy.11.lr, f32[512,8192]{1,0:T(8,128)} %bitcast.12, f32[8192,512]{1,0:T(8,128)} %bitcast.13, f32[512,8192]{1,0:T(8,128)} %bitcast.14, ...), custom_call_target="tpu_custom_call" | custom-call | flops 137438953472 | bytes 134217728 | tf_op jit(solution)/shard_map/sync_kernel/pallas_call | solution.py:363
  387.4 17.5 %finish_kernel.1 = (f32[512,8192]{1,0:T(8,128)}, f32[8192,512]{1,0:T(8,128)}, bf16[2048,2048]{1,0:T(8,128)(2,1)}) custom-call(bf16[2048,2048]{1,0:T(8,128)(2,1)} %get-tuple-element.9.y_hbm, f32[512,8192]{1,0:T(8,128)} %get-tuple-element.10.nw_up, f32[8192,512]{1,0:T(8,128)} %get-tuple-element.11.nw_dn), custom_call_target="tpu_custom_call" | custom-call | bytes 83886080 | tf_op jit(solution)/shard_map/finish_kernel/pallas_call | solution.py:392

commit v3 on v2

v3 whole, which is shorter than its diff:
```python
import functools

import jax
import jax.numpy as jnp
from jax import lax
from jax.experimental import pallas as pl
from jax.experimental.pallas import tpu as pltpu
from jax.sharding import PartitionSpec as P

MESH = pl.DeviceIdType.MESH
COLS = 256
SENDS = 4
TILE = 1024
HALF = COLS // 2
VMEM_SYNC = 16 * 1024 * 1024
VMEM_FINISH = 16 * 1024 * 1024


def gelu(x):
    return 0.5 * x * (1.0 + lax.erf(x * 0.7071067811865476))


def sync_kernel(lr, w_up, w_dn, g_up, g_dn, s_up, s_dn, x_hbm,
                land_up, land_dn, x_v, acc, new_dn, u_v, sb_dn, last_dn,
                wb_up, wb_dn, gb_up, gb_dn, d_up, d_dn, sb_up, lb_up, lb_dn, wg_up, wg_dn,
                t_sem, send_sem, s_sem, l_sem, x_sem,
                y_recv, x_recv, o_recv, n_recv, x_send, o_send, n_send,
                yt_recv, xt_recv, ot_recv, nt_recv, xt_send, ot_send, nt_send):
    side, rep = lax.axis_index("side"), lax.axis_index("rep")
    other = 1 - side
    sib = rep + 1 - 2 * (rep % 2)
    cross = (rep + 2) % 4
    sib_cross = (sib + 2) % 4
    chunks = land_up.shape[0]
    depth = w_up.shape[0]
    tokens, width = x_v.shape
    lands, smalls = (land_up, land_dn), (d_up, d_dn)
    last = chunks - 1

    barrier = pltpu.get_barrier_semaphore()
    for dev in ((other, rep), (side, sib), (side, cross)):
        pl.semaphore_signal(barrier, inc=1, device_id=dev, device_id_type=MESH)

    def span(m):
        return pl.ds(pl.multiple_of(m * COLS, COLS), COLS)

    def late(row, q):
        return last_dn.at[row, pl.ds(q * HALF, HALF), :]

    @pl.when(side == 0)
    def trainer():
        mats = ((w_up, g_up, wb_up, gb_up), (w_dn, g_dn, wb_dn, gb_dn))

        def part(h, ref, m):
            return ref.at[:, span(m)] if h == 0 else ref.at[span(m), :]

        def loads(h, m):
            w, g, wb, gb = mats[h]
            k = m % 2
            return [
                pltpu.make_async_copy(part(h, w, m), wb.at[k], t_sem.at[2 * h, k]),
                pltpu.make_async_copy(part(h, g, m), gb.at[k], t_sem.at[2 * h + 1, k]),
            ]

        def send(h, m):
            return pltpu.make_async_remote_copy(
                src_ref=smalls[h].at[m % SENDS], dst_ref=lands[h].at[m, rep],
                send_sem=send_sem.at[h, m % SENDS], recv_sem=y_recv.at[h, m],
                device_id=(other, rep), device_id_type=MESH)

        def send_late(q):
            m = last - 1 + q // 2
            return pltpu.make_async_remote_copy(
                src_ref=d_dn.at[m % SENDS, pl.ds((q % 2) * HALF, HALF), :], dst_ref=late(rep, q),
                send_sem=xt_send.at[q], recv_sem=yt_recv.at[q],
                device_id=(other, rep), device_id_type=MESH)

        for m in range(2):
            for h in range(2):
                for c in loads(h, m):
                    c.start()
        rate = lr[0]

        def make(h, m):
            k = m % 2
            for c in loads(h, m):
                c.wait()

            @pl.when(m >= SENDS)
            def _():
                send(h, m - SENDS).wait_send()
            old = mats[h][2][k]
            new = old - rate * mats[h][3][k]
            if h == 0:
                acc[:, span(m)] = new
            else:
                new_dn[span(m), :] = new
            smalls[h][m % SENDS] = (new - old).astype(jnp.bfloat16)

            @pl.when(m + 2 < chunks)
            def _():
                for c in loads(h, m + 2):
                    c.start()

        make(0, 0)
        pl.semaphore_wait(barrier, 3)

        def step(m, _):
            make(0, m + 1)

            @pl.when(m == 0)
            def _():
                send(0, 0).start()

            @pl.when(m >= 1)
            def _():
                send(1, m - 1).start()
            make(1, m)
            send(0, m + 1).start()
            return 0

        lax.fori_loop(0, last, step, 0)
        make(1, last)
        for q in range(4):
            send_late(q).start()
        for m in range(chunks - SENDS, chunks):
            send(0, m).wait_send()
        for m in range(chunks - SENDS, last - 1):
            send(1, m).wait_send()
        for q in range(4):
            send_late(q).wait_send()

    @pl.when(side == 1)
    def generator():
        def hop(h, m, row, dev, send, recv):
            return pltpu.make_async_remote_copy(
                src_ref=lands[h].at[m, row], dst_ref=lands[h].at[m, row],
                send_sem=send.at[h, m], recv_sem=recv.at[h, m],
                device_id=(side, dev), device_id_type=MESH)

        def from_trainer(h, m):
            return hop(h, m, rep, sib, x_send, y_recv)

        def across(h, m, row):
            return hop(h, m, row, cross, x_send, x_recv)

        def own(h, m, row):
            return hop(h, m, row, sib, o_send, o_recv)

        def next_own(h, m, row):
            return hop(h, m, row, sib, n_send, n_recv)

        def late_hop(q, row, dev, send, recv):
            return pltpu.make_async_remote_copy(
                src_ref=late(row, q), dst_ref=late(row, q), send_sem=send.at[q], recv_sem=recv.at[q],
                device_id=(side, dev), device_id_type=MESH)

        stales = (sb_up, sb_dn)

        def stale(h, m):
            src = s_up.at[:, span(m)] if h == 0 else s_dn.at[span(m), :]
            return pltpu.make_async_copy(src, stales[h].at[m % 2], s_sem.at[h, m % 2])

        def landed(h, m):
            return pltpu.make_async_copy(lands[h].at[m], (lb_up, lb_dn)[h], l_sem.at[h])

        x_in = pltpu.make_async_copy(x_hbm, x_v, x_sem.at[0])
        x_in.start()
        for m in range(2):
            for h in range(2):
                stale(h, m).start()
        pl.semaphore_wait(barrier, 3)

        def pass_on(h, m):
            from_trainer(h, m).wait_recv()
            across(h, m, rep).start()
            own(h, m, rep).start()

        def pass_late(q):
            late_hop(q, rep, sib, xt_send, yt_recv).wait_recv()
            late_hop(q, rep, cross, xt_send, xt_recv).start()
            late_hop(q, rep, sib, ot_send, ot_recv).start()

        def turn(h, m):
            across(h, m, cross).wait_recv()
            next_own(h, m, cross).start()

        def turn_late(q):
            late_hop(q, cross, cross, xt_send, xt_recv).wait_recv()
            late_hop(q, cross, sib, nt_send, nt_recv).start()

        def fetch(h, m):
            own(h, m, sib).wait_recv()
            next_own(h, m, sib_cross).wait_recv()
            landed(h, m).start()

        tiles = tokens // TILE
        groups = TILE // depth

        def tile_rows(i):
            return pl.ds(pl.multiple_of(i * TILE, TILE), TILE)

        def u_cols(m):
            return pl.ds(pl.multiple_of((m % 2) * COLS, COLS), COLS)

        def up(m):
            k = m % 2
            stale(0, m).wait()
            landed(0, m).wait()
            for r in range(4):
                rows = pl.ds(r * depth, depth)
                wg_up[rows, :] = (sb_up[k, rows, :].astype(jnp.float32) + lb_up[r].astype(jnp.float32)).astype(jnp.bfloat16)

            @pl.when(m + 2 < chunks)
            def _():
                stale(0, m + 2).start()

            def tile(i, _):
                pre = jnp.dot(x_v[tile_rows(i), :], wg_up[...], preferred_element_type=jnp.float32)
                u_v[tile_rows(i), u_cols(m)] = gelu(pre).astype(jnp.bfloat16)
                return 0
            lax.fori_loop(0, tiles, tile, 0)

        def down(m):
            k = m % 2
            stale(1, m).wait()
            landed(1, m).wait()
            for r in range(4):
                cols = pl.ds(r * depth, depth)
                wg_dn[:, cols] = (sb_dn[k, :, cols].astype(jnp.float32) + lb_dn[r].astype(jnp.float32)).astype(jnp.bfloat16)

            @pl.when(m + 2 < chunks)
            def _():
                stale(1, m + 2).start()

            def tile(i, _):
                p = jnp.dot(u_v[tile_rows(i), u_cols(m)], wg_dn[...], preferred_element_type=jnp.float32)
                for g in range(groups):
                    cols = pl.ds(pl.multiple_of((i * groups + g) * width, width), width)
                    acc[:, cols] += p[g * depth:(g + 1) * depth]
                return 0
            lax.fori_loop(0, tiles, tile, 0)

        pass_on(0, 0)
        x_in.wait()

        def clear(i, _):
            cols = pl.ds(pl.multiple_of(i * width, width), width)
            rows = pl.ds(pl.multiple_of(i * depth, depth), depth)
            acc[:, cols] = x_v[rows, :].astype(jnp.float32)
            return 0
        lax.fori_loop(0, tokens // depth, clear, 0)

        def step(m, _):
            pass_on(0, m)
            turn(0, m - 1)

            @pl.when(m >= 3)
            def _():
                down(m - 3)
            fetch(0, m - 1)
            pass_on(1, m - 1)

            @pl.when(m >= 2)
            def _():
                turn(1, m - 2)
            up(m - 1)

            @pl.when(m >= 2)
            def _():
                fetch(1, m - 2)
            return 0

        lax.fori_loop(1, last, step, 0)
        pass_on(0, last)
        turn(0, last - 1)
        down(last - 3)
        fetch(0, last - 1)
        pass_late(0)
        turn(1, last - 2)
        up(last - 1)
        pass_late(1)
        fetch(1, last - 2)
        turn(0, last)
        pass_late(2)
        down(last - 2)
        fetch(0, last)
        pass_late(3)
        turn_late(0)
        up(last)
        for q in range(1, 4):
            turn_late(q)
        for m in range(last - 1, chunks):
            stale(1, m).wait()

        def drain(m, _):
            across(0, m, rep).wait_send()
            own(0, m, rep).wait_send()
            next_own(0, m, cross).wait_send()

            @pl.when(m < last - 1)
            def _():
                across(1, m, rep).wait_send()
                own(1, m, rep).wait_send()
                next_own(1, m, cross).wait_send()
            return 0
        lax.fori_loop(0, chunks, drain, 0)
        for q in range(4):
            late_hop(q, sib, sib, ot_send, ot_recv).wait_recv()
            late_hop(q, sib_cross, sib, nt_send, nt_recv).wait_recv()
        for q in range(4):
            late_hop(q, rep, cross, xt_send, xt_recv).wait_send()
            late_hop(q, rep, sib, ot_send, ot_recv).wait_send()
            late_hop(q, cross, sib, nt_send, nt_recv).wait_send()


def finish_kernel(x_v, acc, new_dn, u_v, sb_dn, last_dn, up_out, dn_out, y_out, wg, y_v, zero, sem, y_sem):
    side = lax.axis_index("side")
    depth = acc.shape[0]
    tokens, width = x_v.shape
    n = up_out.shape[1] // width
    rows_dn = dn_out.shape[0] // n
    blocks = tokens // depth
    pieces = width // zero.shape[1]

    def up_piece(i):
        return pl.ds(i * width, width)

    def dn_piece(i):
        return pl.ds(i * rows_dn, rows_dn)

    def y_piece(i):
        return y_out.at[pl.ds(i * depth, depth), :]

    @pl.when(side == 0)
    def trainer():
        copies = []
        for i in range(n):
            copies.append(pltpu.make_async_copy(acc.at[:, up_piece(i)], up_out.at[:, up_piece(i)], sem.at[0, i, 0]))
            copies.append(pltpu.make_async_copy(new_dn.at[dn_piece(i), :], dn_out.at[dn_piece(i), :], sem.at[1, i, 0]))
        for c in copies:
            c.start()
        y_v[0] = jnp.zeros_like(y_v[0])
        ys = [pltpu.make_async_copy(y_v.at[0], y_piece(i), y_sem.at[i]) for i in range(blocks)]
        for c in ys:
            c.start()
        for c in copies + ys:
            c.wait()

    @pl.when(side == 1)
    def generator():
        zero[...] = jnp.zeros_like(zero)
        size = zero.shape[1]
        copies = []
        for i in range(n):
            for j in range(pieces):
                copies.append(pltpu.make_async_copy(
                    zero, up_out.at[:, pl.ds(i * width + j * size, size)], sem.at[0, i, j]))
                copies.append(pltpu.make_async_copy(
                    zero, dn_out.at[pl.ds(i * rows_dn + j * depth, depth), :], sem.at[1, i, j]))
        for k in range(2):
            ks = pl.ds(k * COLS, COLS)
            for r in range(4):
                cols = pl.ds(r * depth, depth)
                wg[ks, cols] = (sb_dn[k, :, cols].astype(jnp.float32) + last_dn[r, ks, :].astype(jnp.float32)).astype(jnp.bfloat16)
        for c in copies:
            c.start()

        def out(i):
            return pltpu.make_async_copy(y_v.at[i], y_out.at[pl.ds(pl.multiple_of(i * depth, depth), depth), :], y_sem.at[i])

        def block(i, _):
            rows = pl.ds(pl.multiple_of(i * depth, depth), depth)
            cols = pl.ds(pl.multiple_of(i * width, width), width)
            p = jnp.dot(u_v[rows, :], wg[...], preferred_element_type=jnp.float32)
            y_v[i] = (acc[:, cols] + p).astype(jnp.bfloat16)

            @pl.when(i >= 1)
            def _():
                out(i - 1).start()
            return 0
        lax.fori_loop(0, blocks, block, 0)
        for c in copies:
            c.wait()
        out(blocks - 1).start()
        for i in range(blocks):
            out(i).wait()


def step_outputs(lr, w_up, w_dn, g_up, g_dn, s_up, s_dn, x):
    depth, hid = w_up.shape
    tokens, width = x.shape
    chunks = hid // COLS
    any_spec = pl.BlockSpec(memory_space=pltpu.HBM)
    vmem_spec = pl.BlockSpec(memory_space=pltpu.VMEM)
    dma = pltpu.SemaphoreType.DMA
    vmem = pltpu.VMEM
    f32, bf16 = jnp.float32, jnp.bfloat16
    _, _, *held = pl.pallas_call(
        sync_kernel,
        name="sync_kernel",
        out_shape=(
            jax.ShapeDtypeStruct((chunks, 4, depth, COLS), bf16),
            jax.ShapeDtypeStruct((chunks, 4, COLS, depth), bf16),
            vmem((tokens, width), bf16),
            vmem(w_up.shape, f32),
            vmem(w_dn.shape, f32),
            vmem((tokens, 2 * COLS), bf16),
            vmem((2, COLS, width), bf16),
            vmem((4, 2 * COLS, depth), bf16),
        ),
        in_specs=[pl.BlockSpec(memory_space=pltpu.SMEM)] + [any_spec] * 7,
        out_specs=(any_spec,) * 2 + (vmem_spec,) * 6,
        scratch_shapes=[
            vmem((2, depth, COLS), f32), vmem((2, COLS, depth), f32),
            vmem((2, depth, COLS), f32), vmem((2, COLS, depth), f32),
            vmem((SENDS, depth, COLS), bf16), vmem((SENDS, COLS, depth), bf16),
            vmem((2, width, COLS), bf16),
            vmem((4, depth, COLS), bf16), vmem((4, COLS, depth), bf16),
            vmem((width, COLS), bf16), vmem((COLS, width), bf16),
            dma((4, 2)), dma((2, SENDS)), dma((2, 2)), dma((2,)), dma((1,)),
        ] + [dma((2, chunks))] * 7 + [dma((4,))] * 7,
        compiler_params=pltpu.CompilerParams(
            collective_id=0, has_side_effects=True, vmem_limit_bytes=VMEM_SYNC),
        cost_estimate=pl.CostEstimate(flops=4 * tokens * width * hid, bytes_accessed=8 * width * hid, transcendentals=0),
    )(lr, w_up, w_dn, g_up, g_dn, s_up, s_dn, x)
    n = hid // width
    return pl.pallas_call(
        finish_kernel,
        name="finish_kernel",
        out_shape=(
            jax.ShapeDtypeStruct(w_up.shape, f32),
            jax.ShapeDtypeStruct(w_dn.shape, f32),
            jax.ShapeDtypeStruct((tokens, width), bf16),
        ),
        in_specs=[vmem_spec] * 6,
        out_specs=(any_spec,) * 3,
        scratch_shapes=[
            vmem((2 * COLS, width), bf16), vmem((tokens // depth, depth, width), bf16), vmem((depth, depth), f32),
            dma((2, n, width // depth)), dma((tokens // depth,)),
        ],
        compiler_params=pltpu.CompilerParams(vmem_limit_bytes=VMEM_FINISH),
        cost_estimate=pl.CostEstimate(flops=4 * tokens * width * COLS, bytes_accessed=12 * depth * hid, transcendentals=0),
    )(*[pltpu.with_memory_space_constraint(a, pltpu.VMEM) for a in held])


def solution(mesh):
    up_spec = P("side", None, "rep", None)
    down_spec = P("side", None, None, "rep")
    copy_spec = P("side", "rep", None, None, None)
    token_spec = P("side", "rep", None, None)

    def local_step(w_up, w_down, g_up, g_down, learn_rate, old_up, old_down, prompts):
        new_up, new_down, y = step_outputs(
            learn_rate, w_up[0, 0], w_down[0, 0], g_up[0, 0], g_down[0, 0],
            old_up[0, 0, 0], old_down[0, 0, 0], prompts[0, 0])
        return new_up[None, None], new_down[None, None], y[None, None]

    return jax.shard_map(
        local_step,
        mesh=mesh,
        in_specs=(up_spec, down_spec, up_spec, down_spec, P(None), copy_spec, copy_spec, token_spec),
        out_specs=(up_spec, down_spec, token_spec),
        check_vma=False,
    )
```

time: 406 us -> 391 us (0.963)
  Pallas kernels: 404 us -> 390 us
    pallas_call x1, Pallas kernels: 386 us -> 376 us  [step_outputs(): pl.pallas_call(sync_kernel, name='sync_kernel', out_shape=(jax.ShapeDtype...]
where the time goes in v3:
time: 391 us
  Pallas kernels  390 us (100%)
    pallas_call x1, Pallas kernels, step_outputs(): pl.pallas_call(sync_kernel, name='sync_kernel', out_shape=(jax.ShapeDtype...  376 us
    pallas_call x1, Pallas kernels, step_outputs(): pl.pallas_call(finish_kernel, name='finish_kernel', out_shape=(jax.ShapeD...  13.8 us

profile of v3, /device:TPU:5, one launch (start us, length us, event | category | flops | bytes accessed | tf_op | source)
XLA Modules:
  0.0 391.2 jit_solution(4918392007542044783)
XLA Ops:
  1.3 376.0 %sync_kernel.1 = (bf16[32,4,512,256]{3,2,1,0:T(8,128)(2,1)}, bf16[32,4,256,512]{3,2,1,0:T(8,128)(2,1)}, bf16[2048,2048]{1,0:T(8,128)(2,1)S(1)}, f32[512,8192]{1,...) custom-call(f32[1]{0:T(128)S(6)} %copy.11.lr, ...), custom_call_target="tpu_custom_call" | custom-call | flops 137438953472 | bytes 134217728 | tf_op jit(solution)/shard_map/sync_kernel/pallas_call | solution.py:399
  377.3 13.8 %finish_kernel.1 = (f32[512,8192]{1,0:T(8,128)}, f32[8192,512]{1,0:T(8,128)}, bf16[2048,2048]{1,0:T(8,128)(2,1)}) custom-call(bf16[2048,2048]{1,0:T(8,128)(2,1)S(1)} %get-tuple-element.12.x_v, f32[512,8192]{1,0:T(8,128)S(1)} %get-tuple-element.13.acc, f32[8192,512]{1,0:T(8,128)S(1)} %get-tuple-element.14.new_dn, ...), custom_call_target="tpu_custom_call" | custom-call | flops 4294967296 | bytes 50331648 | tf_op jit(solution)/shard_map/finish_kernel/pallas_call | solution.py:428

commit v4 on v3

--- a/solution.py
+++ b/solution.py
@@ -12,20 +12,20 @@
 SENDS = 4
 TILE = 1024
 HALF = COLS // 2
-VMEM_SYNC = 16 * 1024 * 1024
-VMEM_FINISH = 16 * 1024 * 1024
+VMEM_SYNC = 14 * 1024 * 1024
+VMEM_FINISH = 14 * 1024 * 1024
 
 
 def gelu(x):
     return 0.5 * x * (1.0 + lax.erf(x * 0.7071067811865476))
 
 
-def sync_kernel(lr, w_up, w_dn, g_up, g_dn, s_up, s_dn, x_hbm,
-                land_up, land_dn, x_v, acc, new_dn, u_v, sb_dn, last_dn,
-                wb_up, wb_dn, gb_up, gb_dn, d_up, d_dn, sb_up, lb_up, lb_dn, wg_up, wg_dn,
-                t_sem, send_sem, s_sem, l_sem, x_sem,
+def sync_kernel(lr_hbm, w_up, w_dn, g_up, g_dn, s_up, s_dn, x_hbm,
+                land_up, land_dn, x_v, acc, new_dn, u_v, sb_up, sb_dn, last_dn, zero,
+                wb_up, wb_dn, gb_up, gb_dn, d_up, d_dn, swap_dn, lb_up, lb_dn, wg_up, wg_dn,
+                lr, t_sem, send_sem, s_sem, l_sem, x_sem,
                 y_recv, x_recv, o_recv, n_recv, x_send, o_send, n_send,
-                yt_recv, xt_recv, ot_recv, nt_recv, xt_send, ot_send, nt_send):
+                yt_recv, xt_recv, ot_recv, nt_recv, xt_send, ot_send, nt_send, swap_sem):
     side, rep = lax.axis_index("side"), lax.axis_index("rep")
     other = 1 - side
     sib = rep + 1 - 2 * (rep % 2)
@@ -75,10 +75,20 @@
                 send_sem=xt_send.at[q], recv_sem=yt_recv.at[q],
                 device_id=(other, rep), device_id_type=MESH)
 
-        for m in range(2):
-            for h in range(2):
-                for c in loads(h, m):
-                    c.start()
+        swap = pltpu.make_async_remote_copy(
+            src_ref=d_dn.at[last % SENDS, pl.ds(HALF, HALF), :], dst_ref=swap_dn,
+            send_sem=swap_sem.at[0], recv_sem=swap_sem.at[1],
+            device_id=(side, cross), device_id_type=MESH)
+        send_swapped = pltpu.make_async_remote_copy(
+            src_ref=swap_dn, dst_ref=late(cross, 3),
+            send_sem=xt_send.at[4], recv_sem=yt_recv.at[4],
+            device_id=(other, rep), device_id_type=MESH)
+
+        lr_in = pltpu.make_async_copy(lr_hbm, lr, x_sem.at[0])
+        lr_in.start()
+        for c in loads(0, 0):
+            c.start()
+        lr_in.wait()
         rate = lr[0]
 
         def make(h, m):
@@ -103,14 +113,14 @@
                     c.start()
 
         make(0, 0)
+        for h, m in ((0, 1), (1, 0), (1, 1)):
+            for c in loads(h, m):
+                c.start()
         pl.semaphore_wait(barrier, 3)
+        send(0, 0).start()
 
         def step(m, _):
             make(0, m + 1)
-
-            @pl.when(m == 0)
-            def _():
-                send(0, 0).start()
 
             @pl.when(m >= 1)
             def _():
@@ -123,12 +133,17 @@
         make(1, last)
         for q in range(4):
             send_late(q).start()
+        swap.start()
+        swap.wait_recv()
+        send_swapped.start()
+        swap.wait_send()
         for m in range(chunks - SENDS, chunks):
             send(0, m).wait_send()
         for m in range(chunks - SENDS, last - 1):
             send(1, m).wait_send()
         for q in range(4):
             send_late(q).wait_send()
+        send_swapped.wait_send()
 
     @pl.when(side == 1)
     def generator():
@@ -178,7 +193,8 @@
 
         def pass_late(q):
             late_hop(q, rep, sib, xt_send, yt_recv).wait_recv()
-            late_hop(q, rep, cross, xt_send, xt_recv).start()
+            if q < 3:
+                late_hop(q, rep, cross, xt_send, xt_recv).start()
             late_hop(q, rep, sib, ot_send, ot_recv).start()
 
         def turn(h, m):
@@ -186,7 +202,12 @@
             next_own(h, m, cross).start()
 
         def turn_late(q):
-            late_hop(q, cross, cross, xt_send, xt_recv).wait_recv()
+            if q < 3:
+                late_hop(q, cross, cross, xt_send, xt_recv).wait_recv()
+            else:
+                pltpu.make_async_remote_copy(
+                    src_ref=late(cross, q), dst_ref=late(cross, q), send_sem=xt_send.at[4], recv_sem=yt_recv.at[4],
+                    device_id=(side, sib), device_id_type=MESH).wait_recv()
             late_hop(q, cross, sib, nt_send, nt_recv).start()
 
         def fetch(h, m):
@@ -243,6 +264,7 @@
 
         pass_on(0, 0)
         x_in.wait()
+        zero[...] = jnp.zeros_like(zero)
 
         def clear(i, _):
             cols = pl.ds(pl.multiple_of(i * width, width), width)
@@ -284,14 +306,14 @@
         turn(0, last)
         pass_late(2)
         down(last - 2)
-        fetch(0, last)
         pass_late(3)
-        turn_late(0)
-        up(last)
-        for q in range(1, 4):
+        for q in range(4):
             turn_late(q)
+        stale(0, last).wait()
         for m in range(last - 1, chunks):
             stale(1, m).wait()
+        own(0, last, sib).wait_recv()
+        next_own(0, last, sib_cross).wait_recv()
 
         def drain(m, _):
             across(0, m, rep).wait_send()
@@ -309,12 +331,14 @@
             late_hop(q, sib, sib, ot_send, ot_recv).wait_recv()
             late_hop(q, sib_cross, sib, nt_send, nt_recv).wait_recv()
         for q in range(4):
-            late_hop(q, rep, cross, xt_send, xt_recv).wait_send()
+            if q < 3:
+                late_hop(q, rep, cross, xt_send, xt_recv).wait_send()
             late_hop(q, rep, sib, ot_send, ot_recv).wait_send()
             late_hop(q, cross, sib, nt_send, nt_recv).wait_send()
 
 
-def finish_kernel(x_v, acc, new_dn, u_v, sb_dn, last_dn, up_out, dn_out, y_out, wg, y_v, zero, sem, y_sem):
+def finish_kernel(x_v, acc, new_dn, u_v, sb_up, sb_dn, last_dn, zero, land_up, up_out, dn_out, y_out,
+                  wg_up, wg, y_v, u_last, lb_up, sem, y_sem, l_sem):
     side = lax.axis_index("side")
     depth = acc.shape[0]
     tokens, width = x_v.shape
@@ -349,7 +373,9 @@
 
     @pl.when(side == 1)
     def generator():
-        zero[...] = jnp.zeros_like(zero)
+        last = land_up.shape[0] - 1
+        landed = pltpu.make_async_copy(land_up.at[last], lb_up, l_sem.at[0])
+        landed.start()
         size = zero.shape[1]
         copies = []
         for i in range(n):
@@ -358,13 +384,24 @@
                     zero, up_out.at[:, pl.ds(i * width + j * size, size)], sem.at[0, i, j]))
                 copies.append(pltpu.make_async_copy(
                     zero, dn_out.at[pl.ds(i * rows_dn + j * depth, depth), :], sem.at[1, i, j]))
+        for c in copies:
+            c.start()
         for k in range(2):
             ks = pl.ds(k * COLS, COLS)
             for r in range(4):
                 cols = pl.ds(r * depth, depth)
                 wg[ks, cols] = (sb_dn[k, :, cols].astype(jnp.float32) + last_dn[r, ks, :].astype(jnp.float32)).astype(jnp.bfloat16)
-        for c in copies:
-            c.start()
+        landed.wait()
+        for r in range(4):
+            rows = pl.ds(r * depth, depth)
+            wg_up[rows, :] = (sb_up[last % 2, rows, :].astype(jnp.float32) + lb_up[r].astype(jnp.float32)).astype(jnp.bfloat16)
+
+        def up(i, _):
+            rows = pl.ds(pl.multiple_of(i * TILE, TILE), TILE)
+            pre = jnp.dot(x_v[rows, :], wg_up[...], preferred_element_type=jnp.float32)
+            u_last[rows, :] = gelu(pre).astype(jnp.bfloat16)
+            return 0
+        lax.fori_loop(0, tokens // TILE, up, 0)
 
         def out(i):
             return pltpu.make_async_copy(y_v.at[i], y_out.at[pl.ds(pl.multiple_of(i * depth, depth), depth), :], y_sem.at[i])
@@ -372,7 +409,8 @@
         def block(i, _):
             rows = pl.ds(pl.multiple_of(i * depth, depth), depth)
             cols = pl.ds(pl.multiple_of(i * width, width), width)
-            p = jnp.dot(u_v[rows, :], wg[...], preferred_element_type=jnp.float32)
+            u = jnp.concatenate([u_v[rows, :COLS], u_last[rows, :]], axis=1)
+            p = jnp.dot(u, wg[...], preferred_element_type=jnp.float32)
             y_v[i] = (acc[:, cols] + p).astype(jnp.bfloat16)
 
             @pl.when(i >= 1)
@@ -380,9 +418,11 @@
                 out(i - 1).start()
             return 0
         lax.fori_loop(0, blocks, block, 0)
-        for c in copies:
+        for c in copies[:len(copies) // 2]:
             c.wait()
         out(blocks - 1).start()
+        for c in copies[len(copies) // 2:]:
+            c.wait()
         for i in range(blocks):
             out(i).wait()
 
@@ -396,7 +436,7 @@
     dma = pltpu.SemaphoreType.DMA
     vmem = pltpu.VMEM
     f32, bf16 = jnp.float32, jnp.bfloat16
-    _, _, *held = pl.pallas_call(
+    land_up, _, *held = pl.pallas_call(
         sync_kernel,
         name="sync_kernel",
         out_shape=(
@@ -406,20 +446,22 @@
             vmem(w_up.shape, f32),
             vmem(w_dn.shape, f32),
             vmem((tokens, 2 * COLS), bf16),
+            vmem((2, width, COLS), bf16),
             vmem((2, COLS, width), bf16),
             vmem((4, 2 * COLS, depth), bf16),
+            vmem((depth, depth), f32),
         ),
-        in_specs=[pl.BlockSpec(memory_space=pltpu.SMEM)] + [any_spec] * 7,
-        out_specs=(any_spec,) * 2 + (vmem_spec,) * 6,
+        in_specs=[any_spec] * 8,
+        out_specs=(any_spec,) * 2 + (vmem_spec,) * 8,
         scratch_shapes=[
             vmem((2, depth, COLS), f32), vmem((2, COLS, depth), f32),
             vmem((2, depth, COLS), f32), vmem((2, COLS, depth), f32),
             vmem((SENDS, depth, COLS), bf16), vmem((SENDS, COLS, depth), bf16),
-            vmem((2, width, COLS), bf16),
+            vmem((HALF, depth), bf16),
             vmem((4, depth, COLS), bf16), vmem((4, COLS, depth), bf16),
             vmem((width, COLS), bf16), vmem((COLS, width), bf16),
-            dma((4, 2)), dma((2, SENDS)), dma((2, 2)), dma((2,)), dma((1,)),
-        ] + [dma((2, chunks))] * 7 + [dma((4,))] * 7,
+            pltpu.SMEM((1,), f32), dma((4, 2)), dma((2, SENDS)), dma((2, 2)), dma((2,)), dma((1,)),
+        ] + [dma((2, chunks))] * 7 + [dma((5,))] * 7 + [dma((2,))],
         compiler_params=pltpu.CompilerParams(
             collective_id=0, has_side_effects=True, vmem_limit_bytes=VMEM_SYNC),
         cost_estimate=pl.CostEstimate(flops=4 * tokens * width * hid, bytes_accessed=8 * width * hid, transcendentals=0),
@@ -433,15 +475,17 @@
             jax.ShapeDtypeStruct(w_dn.shape, f32),
             jax.ShapeDtypeStruct((tokens, width), bf16),
         ),
-        in_specs=[vmem_spec] * 6,
+        in_specs=[vmem_spec] * 8 + [any_spec],
         out_specs=(any_spec,) * 3,
         scratch_shapes=[
-            vmem((2 * COLS, width), bf16), vmem((tokens // depth, depth, width), bf16), vmem((depth, depth), f32),
-            dma((2, n, width // depth)), dma((tokens // depth,)),
+            vmem((width, COLS), bf16), vmem((2 * COLS, width), bf16),
+            vmem((tokens // depth, depth, width), bf16),
+            vmem((tokens, COLS), bf16), vmem((4, depth, COLS), bf16),
+            dma((2, n, width // depth)), dma((tokens // depth,)), dma((1,)),
         ],
         compiler_params=pltpu.CompilerParams(vmem_limit_bytes=VMEM_FINISH),
         cost_estimate=pl.CostEstimate(flops=4 * tokens * width * COLS, bytes_accessed=12 * depth * hid, transcendentals=0),
-    )(*[pltpu.with_memory_space_constraint(a, pltpu.VMEM) for a in held])
+    )(*[pltpu.with_memory_space_constraint(a, pltpu.VMEM) for a in held], land_up)
 
 
 def solution(mesh):

time: 391 us -> 388 us (level)
  no operation moved by 1% of the time
where the time goes in v4:
time: 388 us
  Pallas kernels  387 us (100%)
    pallas_call x1, Pallas kernels, step_outputs(): pl.pallas_call(sync_kernel, name='sync_kernel', out_shape=(jax.ShapeDtype...  373 us
    pallas_call x1, Pallas kernels, step_outputs(): pl.pallas_call(finish_kernel, name='finish_kernel', out_shape=(jax.ShapeD...  13.9 us

profile of v4, /device:TPU:5, one launch (start us, length us, event | category | flops | bytes accessed | tf_op | source)
XLA Modules:
  0.0 388.1 jit_solution(7141999788739379829)
XLA Ops:
  1.3 372.7 %sync_kernel.1 = (bf16[32,4,512,256]{3,2,1,0:T(8,128)(2,1)}, bf16[32,4,256,512]{3,2,1,0:T(8,128)(2,1)}, bf16[2048,2048]{1,0:T(8,128)(2,1)S(1)}, f32[512,8192]{1,...) custom-call(f32[1]{0:T(128)S(6)} %copy.11.lr_hbm, ...), custom_call_target="tpu_custom_call" | custom-call | flops 137438953472 | bytes 134217728 | tf_op jit(solution)/shard_map/sync_kernel/pallas_call | solution.py:439
  374.0 13.9 %finish_kernel.1 = (f32[512,8192]{1,0:T(8,128)}, f32[8192,512]{1,0:T(8,128)}, bf16[2048,2048]{1,0:T(8,128)(2,1)}) custom-call(bf16[2048,2048]{1,0:T(8,128)(2,1)S(1)} %get-tuple-element.15.x_v, f32[512,8192]{1,0:T(8,128)S(1)} %get-tuple-element.16.acc, f32[8192,512]{1,0:T(8,128)S(1)} %get-tuple-element.17.new_dn, ...), custom_call_target="tpu_custom_call" | custom-call | flops 4294967296 | bytes 50331648 | tf_op jit(solution)/shard_map/finish_kernel/pallas_call | solution.py:470

commit v5 on v4

--- a/solution.py
+++ b/solution.py
@@ -12,6 +12,7 @@
 SENDS = 4
 TILE = 1024
 HALF = COLS // 2
+SWAP = 160
 VMEM_SYNC = 14 * 1024 * 1024
 VMEM_FINISH = 14 * 1024 * 1024
 
@@ -44,6 +45,9 @@
     def span(m):
         return pl.ds(pl.multiple_of(m * COLS, COLS), COLS)
 
+    def swapped(row):
+        return last_dn.at[row, pl.ds(2 * COLS - SWAP, SWAP), :]
+
     def late(row, q):
         return last_dn.at[row, pl.ds(q * HALF, HALF), :]
 
@@ -76,11 +80,11 @@
                 device_id=(other, rep), device_id_type=MESH)
 
         swap = pltpu.make_async_remote_copy(
-            src_ref=d_dn.at[last % SENDS, pl.ds(HALF, HALF), :], dst_ref=swap_dn,
+            src_ref=d_dn.at[last % SENDS, pl.ds(COLS - SWAP, SWAP), :], dst_ref=swap_dn,
             send_sem=swap_sem.at[0], recv_sem=swap_sem.at[1],
             device_id=(side, cross), device_id_type=MESH)
         send_swapped = pltpu.make_async_remote_copy(
-            src_ref=swap_dn, dst_ref=late(cross, 3),
+            src_ref=swap_dn, dst_ref=swapped(cross),
             send_sem=xt_send.at[4], recv_sem=yt_recv.at[4],
             device_id=(other, rep), device_id_type=MESH)
 
@@ -165,6 +169,16 @@
         def next_own(h, m, row):
             return hop(h, m, row, sib, n_send, n_recv)
 
+        def cross_part(q):
+            first = q * HALF if q < 3 else 2 * COLS - SWAP
+            return pl.ds(first, min(HALF, 2 * COLS - SWAP - first) if q < 3 else SWAP)
+
+        def cross_hop(q, row, dev, send, recv):
+            ref = last_dn.at[row, cross_part(q), :]
+            return pltpu.make_async_remote_copy(
+                src_ref=ref, dst_ref=ref, send_sem=send.at[q], recv_sem=recv.at[q],
+                device_id=(side, dev), device_id_type=MESH)
+
         def late_hop(q, row, dev, send, recv):
             return pltpu.make_async_remote_copy(
                 src_ref=late(row, q), dst_ref=late(row, q), send_sem=send.at[q], recv_sem=recv.at[q],
@@ -194,7 +208,7 @@
         def pass_late(q):
             late_hop(q, rep, sib, xt_send, yt_recv).wait_recv()
             if q < 3:
-                late_hop(q, rep, cross, xt_send, xt_recv).start()
+                cross_hop(q, rep, cross, xt_send, xt_recv).start()
             late_hop(q, rep, sib, ot_send, ot_recv).start()
 
         def turn(h, m):
@@ -203,12 +217,12 @@
 
         def turn_late(q):
             if q < 3:
-                late_hop(q, cross, cross, xt_send, xt_recv).wait_recv()
+                cross_hop(q, cross, cross, xt_send, xt_recv).wait_recv()
             else:
                 pltpu.make_async_remote_copy(
-                    src_ref=late(cross, q), dst_ref=late(cross, q), send_sem=xt_send.at[4], recv_sem=yt_recv.at[4],
+                    src_ref=swapped(cross), dst_ref=swapped(cross), send_sem=xt_send.at[4], recv_sem=yt_recv.at[4],
                     device_id=(side, sib), device_id_type=MESH).wait_recv()
-            late_hop(q, cross, sib, nt_send, nt_recv).start()
+            cross_hop(q, cross, sib, nt_send, nt_recv).start()
 
         def fetch(h, m):
             own(h, m, sib).wait_recv()
@@ -329,12 +343,12 @@
         lax.fori_loop(0, chunks, drain, 0)
         for q in range(4):
             late_hop(q, sib, sib, ot_send, ot_recv).wait_recv()
-            late_hop(q, sib_cross, sib, nt_send, nt_recv).wait_recv()
+            cross_hop(q, sib_cross, sib, nt_send, nt_recv).wait_recv()
         for q in range(4):
             if q < 3:
-                late_hop(q, rep, cross, xt_send, xt_recv).wait_send()
+                cross_hop(q, rep, cross, xt_send, xt_recv).wait_send()
             late_hop(q, rep, sib, ot_send, ot_recv).wait_send()
-            late_hop(q, cross, sib, nt_send, nt_recv).wait_send()
+            cross_hop(q, cross, sib, nt_send, nt_recv).wait_send()
 
 
 def finish_kernel(x_v, acc, new_dn, u_v, sb_up, sb_dn, last_dn, zero, land_up, up_out, dn_out, y_out,
@@ -457,7 +471,7 @@
             vmem((2, depth, COLS), f32), vmem((2, COLS, depth), f32),
             vmem((2, depth, COLS), f32), vmem((2, COLS, depth), f32),
             vmem((SENDS, depth, COLS), bf16), vmem((SENDS, COLS, depth), bf16),
-            vmem((HALF, depth), bf16),
+            vmem((SWAP, depth), bf16),
             vmem((4, depth, COLS), bf16), vmem((4, COLS, depth), bf16),
             vmem((width, COLS), bf16), vmem((COLS, width), bf16),
             pltpu.SMEM((1,), f32), dma((4, 2)), dma((2, SENDS)), dma((2, 2)), dma((2,)), dma((1,)),

time: 388 us -> 388 us (level)
  no operation moved by 1% of the time
where the time goes in v5:
time: 388 us; the launch traced here: 387 us
  Pallas kernels  386 us (99%)
    pallas_call x1, Pallas kernels, step_outputs(): pl.pallas_call(sync_kernel, name='sync_kernel', out_shape=(jax.ShapeDtype...  372 us
    pallas_call x1, Pallas kernels, step_outputs(): pl.pallas_call(finish_kernel, name='finish_kernel', out_shape=(jax.ShapeD...  13.9 us

profile of v5, /device:TPU:5, one launch (start us, length us, event | category | flops | bytes accessed | tf_op | source)
XLA Modules:
  0.0 387.4 jit_solution(8730955743322512664)
XLA Ops:
  1.3 372.0 %sync_kernel.1 = (bf16[32,4,512,256]{3,2,1,0:T(8,128)(2,1)}, bf16[32,4,256,512]{3,2,1,0:T(8,128)(2,1)}, bf16[2048,2048]{1,0:T(8,128)(2,1)S(1)}, f32[512,8192]{1,...) custom-call(f32[1]{0:T(128)S(6)} %copy.11.lr_hbm, ...), custom_call_target="tpu_custom_call" | custom-call | flops 137438953472 | bytes 134217728 | tf_op jit(solution)/shard_map/sync_kernel/pallas_call | solution.py:453
  373.3 13.9 %finish_kernel.1 = (f32[512,8192]{1,0:T(8,128)}, f32[8192,512]{1,0:T(8,128)}, bf16[2048,2048]{1,0:T(8,128)(2,1)}) custom-call(bf16[2048,2048]{1,0:T(8,128)(2,1)S(1)} %get-tuple-element.15.x_v, f32[512,8192]{1,0:T(8,128)S(1)} %get-tuple-element.16.acc, f32[8192,512]{1,0:T(8,128)S(1)} %get-tuple-element.17.new_dn, ...), custom_call_target="tpu_custom_call" | custom-call | flops 4294967296 | bytes 50331648 | tf_op jit(solution)/shard_map/finish_kernel/pallas_call | solution.py:484

commit v6 on v5

--- a/solution.py
+++ b/solution.py
@@ -137,13 +137,15 @@
         make(1, last)
         for q in range(4):
             send_late(q).start()
+        for h in range(2):
+            send(h, chunks - SENDS).wait_send()
         swap.start()
         swap.wait_recv()
         send_swapped.start()
         swap.wait_send()
-        for m in range(chunks - SENDS, chunks):
+        for m in range(chunks - SENDS + 1, chunks):
             send(0, m).wait_send()
-        for m in range(chunks - SENDS, last - 1):
+        for m in range(chunks - SENDS + 1, last - 1):
             send(1, m).wait_send()
         for q in range(4):
             send_late(q).wait_send()
@@ -376,9 +378,9 @@
         for i in range(n):
             copies.append(pltpu.make_async_copy(acc.at[:, up_piece(i)], up_out.at[:, up_piece(i)], sem.at[0, i, 0]))
             copies.append(pltpu.make_async_copy(new_dn.at[dn_piece(i), :], dn_out.at[dn_piece(i), :], sem.at[1, i, 0]))
+        y_v[0] = jnp.zeros_like(y_v[0])
         for c in copies:
             c.start()
-        y_v[0] = jnp.zeros_like(y_v[0])
         ys = [pltpu.make_async_copy(y_v.at[0], y_piece(i), y_sem.at[i]) for i in range(blocks)]
         for c in ys:
             c.start()

time: 388 us -> 388 us (level)
  no operation moved by 1% of the time
where the time goes in v6:
time: 388 us; the launch traced here: 387 us
  Pallas kernels  386 us (99%)
    pallas_call x1, Pallas kernels, step_outputs(): pl.pallas_call(sync_kernel, name='sync_kernel', out_shape=(jax.ShapeDtype...  372 us
    pallas_call x1, Pallas kernels, step_outputs(): pl.pallas_call(finish_kernel, name='finish_kernel', out_shape=(jax.ShapeD...  13.9 us

profile of v6, /device:TPU:5, one launch (start us, length us, event | category | flops | bytes accessed | tf_op | source)
XLA Modules:
  0.0 387.4 jit_solution(4192276490080182978)
XLA Ops:
  1.3 372.0 %sync_kernel.1 = (bf16[32,4,512,256]{3,2,1,0:T(8,128)(2,1)}, bf16[32,4,256,512]{3,2,1,0:T(8,128)(2,1)}, bf16[2048,2048]{1,0:T(8,128)(2,1)S(1)}, f32[512,8192]{1,...) custom-call(f32[1]{0:T(128)S(6)} %copy.11.lr_hbm, ...), custom_call_target="tpu_custom_call" | custom-call | flops 137438953472 | bytes 134217728 | tf_op jit(solution)/shard_map/sync_kernel/pallas_call | solution.py:455
  373.3 13.9 %finish_kernel.1 = (f32[512,8192]{1,0:T(8,128)}, f32[8192,512]{1,0:T(8,128)}, bf16[2048,2048]{1,0:T(8,128)(2,1)}) custom-call(bf16[2048,2048]{1,0:T(8,128)(2,1)S(1)} %get-tuple-element.15.x_v, f32[512,8192]{1,0:T(8,128)S(1)} %get-tuple-element.16.acc, f32[8192,512]{1,0:T(8,128)S(1)} %get-tuple-element.17.new_dn, ...), custom_call_target="tpu_custom_call" | custom-call | flops 4294967296 | bytes 50331648 | tf_op jit(solution)/shard_map/finish_kernel/pallas_call | solution.py:486

commit v7 on v6

--- a/solution.py
+++ b/solution.py
@@ -13,8 +13,8 @@
 TILE = 1024
 HALF = COLS // 2
 SWAP = 160
-VMEM_SYNC = 14 * 1024 * 1024
-VMEM_FINISH = 14 * 1024 * 1024
+VMEM_SYNC = 13 * 1024 * 1024
+VMEM_FINISH = 13 * 1024 * 1024
 
 
 def gelu(x):
@@ -22,8 +22,8 @@
 
 
 def sync_kernel(lr_hbm, w_up, w_dn, g_up, g_dn, s_up, s_dn, x_hbm,
-                land_up, land_dn, x_v, acc, new_dn, u_v, sb_up, sb_dn, last_dn, zero,
-                wb_up, wb_dn, gb_up, gb_dn, d_up, d_dn, swap_dn, lb_up, lb_dn, wg_up, wg_dn,
+                land_up, land_dn, x_v, acc, new_dn, u_v, sb_up, sb_dn, last_dn, zero, lb_up,
+                wb_up, wb_dn, gb_up, gb_dn, d_up, d_dn, swap_dn, lb_dn, wg_up, wg_dn,
                 lr, t_sem, send_sem, s_sem, l_sem, x_sem,
                 y_recv, x_recv, o_recv, n_recv, x_send, o_send, n_send,
                 yt_recv, xt_recv, ot_recv, nt_recv, xt_send, ot_send, nt_send, swap_sem):
@@ -323,13 +323,13 @@
         pass_late(2)
         down(last - 2)
         pass_late(3)
+        fetch(0, last)
         for q in range(4):
             turn_late(q)
         stale(0, last).wait()
         for m in range(last - 1, chunks):
             stale(1, m).wait()
-        own(0, last, sib).wait_recv()
-        next_own(0, last, sib_cross).wait_recv()
+        landed(0, last).wait()
 
         def drain(m, _):
             across(0, m, rep).wait_send()
@@ -353,8 +353,8 @@
             cross_hop(q, cross, sib, nt_send, nt_recv).wait_send()
 
 
-def finish_kernel(x_v, acc, new_dn, u_v, sb_up, sb_dn, last_dn, zero, land_up, up_out, dn_out, y_out,
-                  wg_up, wg, y_v, u_last, lb_up, sem, y_sem, l_sem):
+def finish_kernel(x_v, acc, new_dn, u_v, sb_up, sb_dn, last_dn, zero, lb_up, up_out, dn_out, y_out,
+                  wg_up, wg, y_v, u_last, sem, y_sem):
     side = lax.axis_index("side")
     depth = acc.shape[0]
     tokens, width = x_v.shape
@@ -389,9 +389,6 @@
 
     @pl.when(side == 1)
     def generator():
-        last = land_up.shape[0] - 1
-        landed = pltpu.make_async_copy(land_up.at[last], lb_up, l_sem.at[0])
-        landed.start()
         size = zero.shape[1]
         copies = []
         for i in range(n):
@@ -407,10 +404,9 @@
             for r in range(4):
                 cols = pl.ds(r * depth, depth)
                 wg[ks, cols] = (sb_dn[k, :, cols].astype(jnp.float32) + last_dn[r, ks, :].astype(jnp.float32)).astype(jnp.bfloat16)
-        landed.wait()
         for r in range(4):
             rows = pl.ds(r * depth, depth)
-            wg_up[rows, :] = (sb_up[last % 2, rows, :].astype(jnp.float32) + lb_up[r].astype(jnp.float32)).astype(jnp.bfloat16)
+            wg_up[rows, :] = (sb_up[1, rows, :].astype(jnp.float32) + lb_up[r].astype(jnp.float32)).astype(jnp.bfloat16)
 
         def up(i, _):
             rows = pl.ds(pl.multiple_of(i * TILE, TILE), TILE)
@@ -452,7 +448,7 @@
     dma = pltpu.SemaphoreType.DMA
     vmem = pltpu.VMEM
     f32, bf16 = jnp.float32, jnp.bfloat16
-    land_up, _, *held = pl.pallas_call(
+    _, _, *held = pl.pallas_call(
         sync_kernel,
         name="sync_kernel",
         out_shape=(
@@ -466,15 +462,16 @@
             vmem((2, COLS, width), bf16),
             vmem((4, 2 * COLS, depth), bf16),
             vmem((depth, depth), f32),
+            vmem((4, depth, COLS), bf16),
         ),
         in_specs=[any_spec] * 8,
-        out_specs=(any_spec,) * 2 + (vmem_spec,) * 8,
+        out_specs=(any_spec,) * 2 + (vmem_spec,) * 9,
         scratch_shapes=[
             vmem((2, depth, COLS), f32), vmem((2, COLS, depth), f32),
             vmem((2, depth, COLS), f32), vmem((2, COLS, depth), f32),
             vmem((SENDS, depth, COLS), bf16), vmem((SENDS, COLS, depth), bf16),
             vmem((SWAP, depth), bf16),
-            vmem((4, depth, COLS), bf16), vmem((4, COLS, depth), bf16),
+            vmem((4, COLS, depth), bf16),
             vmem((width, COLS), bf16), vmem((COLS, width), bf16),
             pltpu.SMEM((1,), f32), dma((4, 2)), dma((2, SENDS)), dma((2, 2)), dma((2,)), dma((1,)),
         ] + [dma((2, chunks))] * 7 + [dma((5,))] * 7 + [dma((2,))],
@@ -491,17 +488,17 @@
             jax.ShapeDtypeStruct(w_dn.shape, f32),
             jax.ShapeDtypeStruct((tokens, width), bf16),
         ),
-        in_specs=[vmem_spec] * 8 + [any_spec],
+        in_specs=[vmem_spec] * 9,
         out_specs=(any_spec,) * 3,
         scratch_shapes=[
             vmem((width, COLS), bf16), vmem((2 * COLS, width), bf16),
             vmem((tokens // depth, depth, width), bf16),
-            vmem((tokens, COLS), bf16), vmem((4, depth, COLS), bf16),
-            dma((2, n, width // depth)), dma((tokens // depth,)), dma((1,)),
+            vmem((tokens, COLS), bf16),
+            dma((2, n, width // depth)), dma((tokens // depth,)),
         ],
         compiler_params=pltpu.CompilerParams(vmem_limit_bytes=VMEM_FINISH),
         cost_estimate=pl.CostEstimate(flops=4 * tokens * width * COLS, bytes_accessed=12 * depth * hid, transcendentals=0),
-    )(*[pltpu.with_memory_space_constraint(a, pltpu.VMEM) for a in held], land_up)
+    )(*[pltpu.with_memory_space_constraint(a, pltpu.VMEM) for a in held])
 
 
 def solution(mesh):

time: 388 us -> 388 us (level)
  no operation moved by 1% of the time
where the time goes in v7:
time: 388 us; the launch traced here: 387 us
  Pallas kernels  386 us (99%)
    pallas_call x1, Pallas kernels, step_outputs(): pl.pallas_call(sync_kernel, name='sync_kernel', out_shape=(jax.ShapeDtype...  372 us
    pallas_call x1, Pallas kernels, step_outputs(): pl.pallas_call(finish_kernel, name='finish_kernel', out_shape=(jax.ShapeD...  13.9 us

profile of v7, /device:TPU:5, one launch (start us, length us, event | category | flops | bytes accessed | tf_op | source)
XLA Modules:
  0.0 387.4 jit_solution(11314660617380587556)
XLA Ops:
  1.3 372.0 %sync_kernel.1 = (bf16[32,4,512,256]{3,2,1,0:T(8,128)(2,1)}, bf16[32,4,256,512]{3,2,1,0:T(8,128)(2,1)}, bf16[2048,2048]{1,0:T(8,128)(2,1)S(1)}, f32[512,8192]{1,...) custom-call(f32[1]{0:T(128)S(6)} %copy.11.lr_hbm, ...), custom_call_target="tpu_custom_call" | custom-call | flops 137438953472 | bytes 134217728 | tf_op jit(solution)/shard_map/sync_kernel/pallas_call | solution.py:451
  373.3 13.9 %finish_kernel.1 = (f32[512,8192]{1,0:T(8,128)}, f32[8192,512]{1,0:T(8,128)}, bf16[2048,2048]{1,0:T(8,128)(2,1)}) custom-call(bf16[2048,2048]{1,0:T(8,128)(2,1)S(1)} %get-tuple-element.15.x_v, f32[512,8192]{1,0:T(8,128)S(1)} %get-tuple-element.16.acc, f32[8192,512]{1,0:T(8,128)S(1)} %get-tuple-element.17.new_dn, ...), custom_call_target="tpu_custom_call" | custom-call | flops 4294967296 | bytes 50331648 | tf_op jit(solution)/shard_map/finish_kernel/pallas_call | solution.py:483
